TPU v7x, 32 devices: a whole 2x2x4 slice. The times are simulated.
32 devices in a mesh: rep: 1, dp: 32 (over x, y, z, core).
Axes of the slice: x: 2, y: 2, z: 4, core: 2. Of those that a mesh axis runs over, the one named last changes fastest.
Arguments:
- x: bfloat16 [32, 2048, 1024], P(('rep', 'dp'))
- dy: bfloat16 [32, 2048, 1024], P(('rep', 'dp'))
- w_gate: bfloat16 [2, 1024, 2560], replicated
- w_up: bfloat16 [2, 1024, 2560], replicated
- w_down: bfloat16 [2, 2560, 1024], replicated
- m_w_gate: float32 [2, 1024, 2560], replicated
- m_w_up: float32 [2, 1024, 2560], replicated
- m_w_down: float32 [2, 2560, 1024], replicated
- v_w_gate: float32 [2, 1024, 2560], replicated
- v_w_up: float32 [2, 1024, 2560], replicated
- v_w_down: float32 [2, 2560, 1024], replicated
Outputs:
- output 1: bfloat16 [2, 1024, 2560], P('rep')
- output 2: bfloat16 [2, 1024, 2560], P('rep')
- output 3: bfloat16 [2, 2560, 1024], P('rep')
- output 4: float32 [2, 1024, 2560], P('rep')
- output 5: float32 [2, 1024, 2560], P('rep')
- output 6: float32 [2, 2560, 1024], P('rep')
- output 7: float32 [2, 1024, 2560], P('rep')
- output 8: float32 [2, 1024, 2560], P('rep')
- output 9: float32 [2, 2560, 1024], P('rep')
All inputs are finite; a program needn't handle non-finite values.
Results may differ from a plain program's by a relative error of at most 0.022.
Values are sent between devices in bfloat16 or wider.
A program may use at most 2.5 GiB of HBM per device.

v0:
```python
import jax
import jax.numpy as jnp
from jax import lax
from jax.sharding import PartitionSpec as P

NAMES = ("w_gate", "w_up", "w_down")


def matmul(a, w):
    return jnp.dot(a, w, preferred_element_type=jnp.float32).astype(jnp.bfloat16)


def normed(h):
    wide = h.astype(jnp.float32)
    scale = lax.rsqrt(jnp.mean(wide**2, -1, keepdims=True) + 1e-6)
    return (wide * scale).astype(jnp.bfloat16)


def layer(h, w):
    a = normed(h)
    gate = jnp.dot(a, w["w_gate"], preferred_element_type=jnp.float32)
    up = jnp.dot(a, w["w_up"], preferred_element_type=jnp.float32)
    return h + matmul((jax.nn.silu(gate) * up).astype(jnp.bfloat16), w["w_down"])


def adamw(w, m, v, g):
    m = 0.9 * m + 0.1 * g
    v = 0.95 * v + 0.05 * g * g
    step = m * lax.rsqrt(v + 1e-8) + 0.1 * w
    return (w - 0.02 * step).astype(jnp.bfloat16), m, v


def clipped(gradients, sum_of_squares, count):
    factor = jnp.minimum(1.0, 0.5 * lax.rsqrt(sum_of_squares / count + 1e-30))
    return [g * factor for g in gradients]


def solution(mesh):
    def step(x, dy, *arrays):
        weights, m, v = (arrays[i : i + 3] for i in (0, 3, 6))
        layers = weights[0].shape[0]
        h, kept = x[0], []
        for number in range(layers):
            kept.append(h)
            h = layer(h, {name: w[number] for name, w in zip(NAMES, weights, strict=True)})
        by_h, summed = dy[0], [None] * layers
        for number in reversed(range(layers)):
            _, back = jax.vjp(lambda w, h: layer(h, w), {name: w[number] for name, w in zip(NAMES, weights, strict=True)}, kept[number])
            by_w, by_h = back(by_h)
            summed[number] = [lax.psum(by_w[name], "dp") for name in NAMES]
        gradients = [jnp.stack([summed[number][i] for number in range(layers)]).astype(jnp.float32) for i in range(3)]
        gradients = clipped(gradients, sum(jnp.sum(g * g) for g in gradients), sum(g.size for g in gradients))
        new = [adamw(w.astype(jnp.float32), m, v, g) for w, m, v, g in zip(weights, m, v, gradients, strict=True)]
        return tuple(one[which] for which in range(3) for one in new)

    return jax.shard_map(
        step,
        mesh=mesh,
        in_specs=(P(("rep", "dp"), None, None),) * 2 + (P(None, None, None),) * 9,
        out_specs=(P("rep", None, None),) * 9,
        check_vma=False,
    )
```

profile of v0, /device:TPU:25, one launch (start us, length us, event | category | flops | bytes accessed | tf_op | source)
XLA Modules:
  0.0 939.9 jit_solution(9438999075193718423)
XLA Ops:
  7.2 0.0 all-reduce.3.cloned.1.call-start
  7.2 6.5 copy.20
  13.7 3.1 fusion.36
  16.8 0.0 slice-start.2
  16.8 6.7 copy.21
  23.5 16.9 %convolution_convert_fusion.1 = bf16[2048,2560]{1,0:T(8,128)(2,1)} fusion(bf16[2,2560,1024]{2,1,0:T(8,128)(2,1)} %param.15, bf16[1,2048,1024]{2,1,0:T(8,128)(2,1)} %param.12), kind=kOutput, calls=%fused_computation.63 | convolution fusion | flops 10742661120 | bytes 19922944 | tf_op jit(solution)/shard_map/transpose(jvp())/dot_general | solution.py:10
  40.4 0.0 slice-done.2
  40.4 0.0 slice-done.3
  40.4 0.0 slice-done.4
  40.4 14.1 %fusion.62 = f32[2048,2560]{1,0:T(8,128)} fusion(bf16[2,1024,2560]{2,1,0:T(8,128)(2,1)S(1)} %bitcast.77, bf16[1,2048,1024]{2,1,0:T(8,128)(2,1)S(1)} %copy-done.4, f32[2048]{0:T(1024)S(1)} %add_rsqrt_fusion), kind=kOutput, calls=%fused_computation.99 | convolution fusion | flops 10743709696 | bytes 30416896 | tf_op jit(solution)/shard_map/dot_general | solution.py:21
  54.5 0.0 copy-done.7
  54.5 26.7 %multiply_convert_fusion.1 = (bf16[2048,2560]{1,0:T(8,128)(2,1)}, f32[2048,2560]{1,0:T(8,128)}) fusion(f32[2048,2560]{1,0:T(8,128)} %fusion.62, bf16[2,1024,2560]{2,1,0:T(8,128)(2,1)} %param.14, bf16[1,2048,1024]{2,1,0:T(8,128)(2,1)} %param.11, f32[2048]{0:T(1024)S(1)} %add_rsqrt_fusion), kind=kOutput, calls=%fused_computation.53 | convolution fusion | flops 10775166976 | bytes 61874176 | tf_op jit(solution)/shard_map/dot_general | solution.py:22
  81.3 17.7 %fusion.40 = (f32[2048]{0:T(1024)S(1)}, bf16[2048,1024]{0,1:T(8,128)(2,1)}) fusion(bf16[2048,2560]{1,0:T(8,128)(2,1)} %get-tuple-element.24, bf16[2,2560,1024]{2,1,0:T(8,128)(2,1)} %param.15, bf16[1,2048,1024]{1,2,0:T(8,128)(2,1)S(1)} %copy-done.2), kind=kOutput, calls=%fused_computation.76 | convolution fusion | flops 10747901952 | bytes 24125440 | tf_op jit(solution)/shard_map/dot_general | solution.py:10
  98.9 18.5 %fusion.49 = f32[2048,2560]{1,0:T(8,128)} fusion(bf16[2,1024,2560]{2,1,0:T(8,128)(2,1)} %param.14, bf16[2048,1024]{0,1:T(8,128)(2,1)} %get-tuple-element.27, f32[2048]{0:T(1024)S(1)} %fusion.98), kind=kOutput, calls=%fused_computation.86 | convolution fusion | flops 10743709696 | bytes 30416896 | tf_op jit(solution)/shard_map/jvp()/dot_general | solution.py:22
  117.4 32.5 %fusion.20 = (bf16[2048,2560]{1,0:T(8,128)(2,1)}, f32[2048,2560]{1,0:T(8,128)}) fusion(f32[2048,2560]{1,0:T(8,128)} %fusion.49, bf16[2048,2560]{1,0:T(8,128)(2,1)} %convolution_convert_fusion.1, bf16[2,1024,2560]{2,1,0:T(8,128)(2,1)} %param.13, bf16[2048,1024]{0,1:T(8,128)(2,1)} %get-tuple-element.27, f32[2048]{0:T(1024)S(1)} %fusion.98), kind=kOutput, calls=%fused_computation.41 | convolution fusion | flops 10806624256 | bytes 72359936 | tf_op jit(solution)/shard_map/jvp()/dot_general | solution.py:21
  149.9 19.9 %fusion.33 = bf16[2048,1024]{0,1:T(8,128)(2,1)} fusion(bf16[2048,2560]{1,0:T(8,128)(2,1)} %convolution_convert_fusion.1, bf16[2,1024,2560]{2,1,0:T(8,128)(2,1)} %param.14, f32[2048,2560]{1,0:T(8,128)} %get-tuple-element.29), kind=kOutput, calls=%fused_computation.61 | convolution fusion | flops 10768875520 | bytes 40894464 | tf_op jit(solution)/shard_map/transpose(jvp())/dot_general | solution.py:22
  169.8 20.0 %fusion.71 = bf16[1,1024,2560]{2,1,0:T(8,128)(2,1)} fusion(bf16[2048,2560]{1,0:T(8,128)(2,1)} %convolution_convert_fusion.1, bf16[2048,1024]{0,1:T(8,128)(2,1)} %get-tuple-element.27, f32[2048]{0:T(1024)S(1)} %fusion.98, f32[2048,2560]{1,0:T(8,128)} %get-tuple-element.29), kind=kOutput, calls=%fused_computation.106 | convolution fusion | flops 10777788416 | bytes 40902656 | tf_op jit(solution)/shard_map/transpose(jvp())/dot_general | solution.py:22
  189.8 22.1 %fusion.72 = bf16[1,2560,1024]{2,1,0:T(8,128)(2,1)} fusion(f32[2048,2560]{1,0:T(8,128)} %fusion.49, bf16[1,2048,1024]{2,1,0:T(8,128)(2,1)} %param.12, f32[2048,2560]{1,0:T(8,128)} %get-tuple-element.29), kind=kOutput, calls=%fused_computation.107 | convolution fusion | flops 10771496960 | bytes 51380224 | tf_op jit(solution)/shard_map/transpose(jvp())/dot_general | solution.py:10
  211.9 16.6 %fusion.73 = bf16[1,1024,2560]{2,1,0:T(8,128)(2,1)} fusion(bf16[2048,2560]{1,0:T(8,128)(2,1)} %get-tuple-element.28, bf16[2048,1024]{0,1:T(8,128)(2,1)} %get-tuple-element.27, f32[2048]{0:T(1024)S(1)} %fusion.98), kind=kOutput, calls=%fused_computation.108 | convolution fusion | flops 10743709696 | bytes 19931136 | tf_op jit(solution)/shard_map/transpose(jvp())/dot_general | solution.py:21
  228.5 16.8 %fusion.42 = (f32[2048]{0:T(1024)S(1)}, bf16[2048,1024]{0,1:T(8,128)(2,1)S(1)}) fusion(bf16[2048,1024]{0,1:T(8,128)(2,1)S(1)} %copy-done.3, bf16[2048,1024]{0,1:T(8,128)(2,1)} %fusion.33, bf16[2048,2560]{1,0:T(8,128)(2,1)} %get-tuple-element.28, bf16[2,1024,2560]{2,1,0:T(8,128)(2,1)} %param.13), kind=kOutput, calls=%fused_computation.78 | convolution fusion | flops 10747901952 | bytes 28319744 | tf_op jit(solution)/shard_map/transpose(jvp())/dot_general | solution.py:21
  245.4 3.2 fusion.82
  248.5 15.8 %convolution_convert_fusion = bf16[2048,2560]{1,0:T(8,128)(2,1)} fusion(bf16[2048,1024]{0,1:T(8,128)(2,1)S(1)} %fusion.82, bf16[2,2560,1024]{2,1,0:T(8,128)(2,1)} %param.15), kind=kOutput, calls=%fused_computation.62 | convolution fusion | flops 10742661120 | bytes 19922944 | tf_op jit(solution)/shard_map/transpose(jvp())/dot_general | solution.py:10
  264.4 15.6 %fusion.74 = bf16[1,2560,1024]{2,1,0:T(8,128)(2,1)} fusion(bf16[2048,2560]{1,0:T(8,128)(2,1)} %get-tuple-element.24, bf16[2048,1024]{0,1:T(8,128)(2,1)S(1)} %fusion.82), kind=kOutput, calls=%fused_computation.109 | convolution fusion | flops 10740039680 | bytes 19922944 | tf_op jit(solution)/shard_map/transpose(jvp())/dot_general | solution.py:10
  280.0 20.0 %fusion.67 = bf16[1,1024,2560]{2,1,0:T(8,128)(2,1)} fusion(bf16[2048,2560]{1,0:T(8,128)(2,1)} %convolution_convert_fusion, bf16[1,2048,1024]{1,2,0:T(8,128)(2,1)} %copy.20, f32[2048]{0:T(1024)S(1)} %copy-done.8, f32[2048,2560]{1,0:T(8,128)} %fusion.62), kind=kOutput, calls=%fused_computation.104 | convolution fusion | flops 10777788416 | bytes 40902656 | tf_op jit(solution)/shard_map/transpose(jvp())/dot_general | solution.py:22
  299.9 25.0 %fusion.68 = bf16[1,1024,2560]{2,1,0:T(8,128)(2,1)} fusion(f32[2048,2560]{1,0:T(8,128)} %fusion.62, f32[2048,2560]{1,0:T(8,128)} %get-tuple-element.25, bf16[2048,2560]{1,0:T(8,128)(2,1)} %convolution_convert_fusion, bf16[1,2048,1024]{1,2,0:T(8,128)(2,1)} %copy.20, f32[2048]{0:T(1024)S(1)} %copy-done.8), kind=kOutput, calls=%fused_computation.105 | convolution fusion | flops 10804002816 | bytes 61874176 | tf_op jit(solution)/shard_map/transpose(jvp())/dot_general | solution.py:21
  324.9 0.0 all-reduce.3.cloned.1.call-update
  324.9 468.7 %all-reduce.3.cloned.1.call-done = (bf16[1,1024,2560]{2,1,0:T(8,128)(2,1)}, bf16[1,1024,2560]{2,1,0:T(8,128)(2,1)}, bf16[1,1024,2560]{2,1,0:T(8,128)(2,1)}, bf16...) async-done(((bf16[1,1024,2560]{2,1,0:T(8,128)(2,1)}, bf16[1,1024,2560]{2,1,0:T(8,128)(2,1)}, ...) | async-done | bytes 31457296 | tf_op jit(solution)/shard_map/psum | solution.py:50
  793.7 9.4 %fusion.10 = f32[]{:T(128)} fusion(bf16[1,1024,2560]{2,1,0:T(8,128)(2,1)} %get-tuple-element.9, bf16[1,1024,2560]{2,1,0:T(8,128)(2,1)} %get-tuple-element.10), kind=kLoop, calls=%fused_computation.31 | loop fusion | flops 20971520 | bytes 10485764 | tf_op jit(solution)/shard_map/reduce_sum | solution.py:52
  803.1 6.0 fusion.11
  810.4 8.5 fusion.12
  819.6 40.1 %fusion.18 = (bf16[2,2560,1024]{2,1,0:T(8,128)(2,1)}, f32[2,2560,1024]{2,1,0:T(8,128)}, f32[2,2560,1024]{2,1,0:T(8,128)}) fusion(bf16[2,2560,1024]{2,1,0:T(8,128)(2,1)} %param.15, f32[]{:T(128)S(6)} %min_shard_map.3, bf16[1,2560,1024]{2,1,0:T(8,128)(2,1)} %get-tuple-element.13, bf16[1,2560,1024]{2,1,0:T(8,128)(2,1)} %get-tuple-element.14, ...), kind=kLoop, calls=%fused_computation.39 | loop fusion | flops 104857600 | bytes 115343360 | tf_op jit(solution)/shard_map/convert_element_type | solution.py:30
  859.8 72.8 %fusion.8 = (bf16[2,1024,2560]{2,1,0:T(8,128)(2,1)}, f32[2,1024,2560]{2,1,0:T(8,128)}, f32[2,1024,2560]{2,1,0:T(8,128)}, bf16[2,1024,2560]{2,1,0:T(8,128)(2,1)},...) fusion(bf16[2,1024,2560]{2,1,0:T(8,128)(2,1)} %param.13, f32[]{:T(128)S(6)} %min_shard_map.3, ...), kind=kLoop, calls=%fused_computation.29 | loop fusion | flops 209715200 | bytes 230686720 | tf_op jit(solution)/shard_map/convert_element_type | solution.py:30
  (28 shorter events, 0.1 us)
Async XLA Ops:
  7.2 786.5 %all-reduce.3.cloned.1.call-start = ((), (), s32[]{:S(2)}) async-start(), calls=%async_computation | async-start | bytes 62914560 | tf_op jit(solution)/shard_map/psum | solution.py:50
  16.8 37.7 %copy-start.7 = (f32[2048]{0:T(1024)}, f32[2048]{0:T(1024)S(1)}, u32[]{:S(2)}) copy-start(f32[2048]{0:T(1024)S(1)} %add_rsqrt_fusion) | copy-start | bytes 24580
  16.8 23.6 %slice-start.2 = ((s8[10485760]{0:T(1024)(128)(4,1)}), s8[2097152]{0:T(1024)(128)(4,1)S(1)}, s32[]{:S(2)}) async-start(s8[10485760]{0:T(1024)(128)(4,1)} %bitcast.76), calls=%async_computation.3 | async-start | bytes 4194304
  23.5 16.9 %slice-start.3 = ((s8[10485760]{0:T(1024)(128)(4,1)}), s8[4194304]{0:T(1024)(128)(4,1)S(1)}, s32[]{:S(2)}) async-start(s8[10485760]{0:T(1024)(128)(4,1)} %bitcast.76), calls=%async_computation.4 | async-start | bytes 8388608
  23.5 16.9 %slice-start.4 = ((s8[10485760]{0:T(1024)(128)(4,1)}), s8[4194304]{0:T(1024)(128)(4,1)S(1)}, s32[]{:S(2)}) async-start(s8[10485760]{0:T(1024)(128)(4,1)} %bitcast.76), calls=%async_computation.5 | async-start | bytes 8388608
  23.5 16.9 %copy-start.4 = (bf16[1,2048,1024]{2,1,0:T(8,128)(2,1)S(1)}, bf16[1,2048,1024]{2,1,0:T(8,128)(2,1)}, u32[]{:S(2)}) copy-start(bf16[1,2048,1024]{2,1,0:T(8,128)(2,1)} %param.11) | copy-start | bytes 12582916
  54.5 26.7 %copy-start.2 = (bf16[1,2048,1024]{1,2,0:T(8,128)(2,1)S(1)}, bf16[1,2048,1024]{1,2,0:T(8,128)(2,1)}, u32[]{:S(2)}) copy-start(bf16[1,2048,1024]{1,2,0:T(8,128)(2,1)} %copy.20) | copy-start | bytes 12582916
  98.9 18.5 %copy-start.5 = (f32[2048]{0:T(1024)}, f32[2048]{0:T(1024)S(1)}, u32[]{:S(2)}) copy-start(f32[2048]{0:T(1024)S(1)} %get-tuple-element.26) | copy-start | bytes 24580
  211.9 16.6 %copy-start.3 = (bf16[2048,1024]{0,1:T(8,128)(2,1)S(1)}, bf16[2048,1024]{0,1:T(8,128)(2,1)}, u32[]{:S(2)}) copy-start(bf16[2048,1024]{0,1:T(8,128)(2,1)} %get-tuple-element.27) | copy-start | bytes 12582916
  228.5 16.8 %copy-start.6 = (f32[2048]{0:T(1024)S(1)}, f32[2048]{0:T(1024)}, u32[]{:S(2)}) copy-start(f32[2048]{0:T(1024)} %copy-done.5) | copy-start | bytes 24580
  228.5 16.9 %copy-start.1 = (bf16[1,2048,1024]{1,2,0:T(8,128)(2,1)S(1)}, bf16[1,2048,1024]{1,2,0:T(8,128)(2,1)}, u32[]{:S(2)}) copy-start(bf16[1,2048,1024]{1,2,0:T(8,128)(2,1)} %copy.21) | copy-start | bytes 12582916
  264.4 15.6 %copy-start.8 = (f32[2048]{0:T(1024)S(1)}, f32[2048]{0:T(1024)}, u32[]{:S(2)}) copy-start(f32[2048]{0:T(1024)} %copy-done.7) | copy-start | bytes 24580
  793.7 9.5 %slice-start = ((s8[5242880]{0:T(1024)(128)(4,1)}), s8[4194304]{0:T(1024)(128)(4,1)S(1)}, s32[]{:S(2)}) async-start(s8[5242880]{0:T(1024)(128)(4,1)} %bitcast.74), calls=%async_computation.1 | async-start | bytes 8388608
  793.7 9.5 %copy-start = (bf16[1,1024,2560]{2,1,0:T(8,128)(2,1)S(1)}, bf16[1,1024,2560]{2,1,0:T(8,128)(2,1)}, u32[]{:S(2)}) copy-start(bf16[1,1024,2560]{2,1,0:T(8,128)(2,1)} %get-tuple-element.12) | copy-start | bytes 15728644
  793.7 9.5 %slice-start.1 = ((s8[5242880]{0:T(1024)(128)(4,1)}), s8[1048576]{0:T(1024)(128)(4,1)S(1)}, s32[]{:S(2)}) async-start(s8[5242880]{0:T(1024)(128)(4,1)} %bitcast.74), calls=%async_computation.2 | async-start | bytes 2097152
Sparse Core Ops, SparseCore 0:
  325.0 468.5 all-reduce.2
where the time goes:
time: 951 us; the launch traced here: 940 us
  waiting for transfers between devices  469 us (49%)
  matrix products  298 us (31%)
  other arithmetic  143 us (15%)
  between operations  16.6 us (2%)
  local copies, waits for them, and re-layouts  13.2 us (1%)
    psum x1, waiting for transfers between devices, step(): summed[number] = [lax.psum(by_w[name], 'dp') for name in NAMES]  469 us
    convert_element_type x2, other arithmetic, adamw(): return ((w - 0.02 * step).astype(jnp.bfloat16), m, v)  113 us
    dot_general x5, matrix products, layer(): up = jnp.dot(a, w['w_up'], preferred_element_type=jnp.float32)  105 us
    dot_general x5, matrix products, layer(): gate = jnp.dot(a, w['w_gate'], preferred_element_type=jnp.float32)  105 us
    dot_general x5, matrix products, matmul(): jnp.dot(a, w, preferred_element_type=jnp.float32).astype(jnp.bfloat16)  88.1 us
    reduce_sum x3, other arithmetic, step(): jnp.sum(g * g)  24 us
  transfers between devices with their start and end apart: 1, of which 1 were waited for; matrix products, arithmetic and copies ran while one was open for 0% of the time, Pallas kernels for 0%

commit v1 on v0

v1 whole, which is shorter than its diff:
```python
import functools

import jax
import jax.numpy as jnp
from jax import lax
from jax.experimental import pallas as pl
from jax.experimental.pallas import tpu as pltpu
from jax.sharding import PartitionSpec as P

NAMES = ("w_gate", "w_up", "w_down")
MESH = pl.DeviceIdType.MESH
LIMIT = 66_000_000
CORE, Z1, Z2, Y, X = 1, 2, 4, 8, 16
ORDERS = ((X, Z1, Y, Z2), (Y, Z1, X, Z2))


def matmul(a, w):
    return jnp.dot(a, w, preferred_element_type=jnp.float32).astype(jnp.bfloat16)


def normed(h):
    wide = h.astype(jnp.float32)
    scale = lax.rsqrt(jnp.mean(wide**2, -1, keepdims=True) + 1e-6)
    return (wide * scale).astype(jnp.bfloat16)


def layer(h, w):
    a = normed(h)
    gate = jnp.dot(a, w["w_gate"], preferred_element_type=jnp.float32)
    up = jnp.dot(a, w["w_up"], preferred_element_type=jnp.float32)
    return h + matmul((jax.nn.silu(gate) * up).astype(jnp.bfloat16), w["w_down"])


def bit_of(me, stride):
    return lax.rem(lax.div(me, stride), 2)


def other(me, stride):
    return me + stride * (1 - 2 * bit_of(me, stride))


def all_reduce_kernel(shapes, n, *refs):
    k = len(shapes)
    grads, outs, sq_out = refs[:k], refs[k : 2 * k], refs[2 * k]
    refs = refs[2 * k + 1 :]
    own, landed, refs = refs[:k], [refs[k + 5 * i : k + 5 * i + 5] for i in range(k)], refs[6 * k :]
    final, sq, (local_sem, send_sem, recv_sem, ag_local, ag_send, ag_recv, sq_send, sq_recv) = refs[:k], refs[k], refs[k + 1 :]
    me = lax.axis_index("dp")
    core = bit_of(me, CORE)

    def remote(src, dst, send, recv, stride):
        return pltpu.make_async_remote_copy(src, dst, send, recv, device_id={"dp": other(me, stride)}, device_id_type=MESH)

    def columns(i, half):
        width = shapes[i][1] // 2
        return pl.ds(half * width, width)

    def starts(i, half):
        size, at = shapes[i][0] // 2, 0
        found = [at]
        for stride in ORDERS[half]:
            size //= 2
            at = at + bit_of(me, stride) * size
            found.append(at)
        return found

    def rs_copy(i, half, stage):
        stride = ORDERS[half][stage - 1]
        size = shapes[i][0] >> (stage + 1)
        at = starts(i, half)[stage - 1] + (1 - bit_of(me, stride)) * size
        cols = columns(i, half)
        return remote(
            own[i].at[pl.ds(pl.multiple_of(at, 16), size), cols],
            landed[i][stage].at[:, cols],
            send_sem.at[i, half, stage],
            recv_sem.at[i, half, stage],
            stride,
        )

    def core_copy(i):
        rows = shapes[i][0] // 2
        away = pl.ds(pl.multiple_of((1 - core) * rows, 16), rows)
        return remote(grads[i].at[away, :], landed[i][0], send_sem.at[i, 0, 0], recv_sem.at[i, 0, 0], CORE)

    def own_copy(i):
        rows = shapes[i][0] // 2
        return pltpu.make_async_copy(grads[i].at[pl.ds(pl.multiple_of(core * rows, 16), rows), :], own[i], local_sem.at[i])

    def summed(i, half, stage, at, row):
        cols, found = columns(i, half), starts(i, half)
        place = lambda start: pl.ds(pl.multiple_of(at - start + row, 16), 16)
        total = own[i][place(0), cols].astype(jnp.float32)
        for s in range(stage + 1):
            total += landed[i][s][place(found[s]), cols].astype(jnp.float32)
        return total

    def rs_step(i, half, stage):
        stride = ORDERS[half][stage - 1]
        size = shapes[i][0] >> (stage + 1)
        at = starts(i, half)[stage - 1] + (1 - bit_of(me, stride)) * size

        @pl.loop(0, size // 16)
        def _(block):
            row = block * 16
            total = summed(i, half, stage - 1, at, row)
            own[i][pl.ds(pl.multiple_of(at + row, 16), 16), columns(i, half)] = total.astype(jnp.bfloat16)

        rs_copy(i, half, stage).start()

    def finish(i, half):
        size, width = shapes[i][0] // 32, shapes[i][1] // 2
        at = starts(i, half)[4]

        @pl.loop(0, size // 16)
        def _(block):
            row = block * 16
            total = summed(i, half, 4, at, row).astype(jnp.bfloat16)
            final[i][pl.ds(pl.multiple_of(row, 16), 16), columns(i, half)] = total
            wide = total.astype(jnp.float32)
            wide = wide * wide
            part = wide[:, :128]
            for j in range(1, width // 128):
                part += wide[:, j * 128 : (j + 1) * 128]
            sq[...] += part

    def region(i, half, stage):
        size = shapes[i][0] >> (stage + 1)
        at = core * (shapes[i][0] // 2) + starts(i, half)[stage]
        return pl.ds(pl.multiple_of(at, 16), size), columns(i, half)

    def ag_copy(i, half, stage):
        rows, cols = region(i, half, stage)
        src = final[i].at[:, cols] if stage == 4 else outs[i].at[rows, cols]
        return remote(
            src, outs[i].at[rows, cols], ag_send.at[i, half, stage], ag_recv.at[i, half, stage], ORDERS[half][stage - 1]
        )

    def ag_own(i, half):
        rows, cols = region(i, half, 4)
        return pltpu.make_async_copy(final[i].at[:, cols], outs[i].at[rows, cols], ag_local.at[i, half])

    def ag_core(i):
        rows = shapes[i][0] // 2
        mine = pl.ds(pl.multiple_of(core * rows, 16), rows)
        return remote(outs[i].at[mine, :], outs[i].at[mine, :], ag_send.at[i, 0, 0], ag_recv.at[i, 0, 0], CORE)

    for i in range(k):
        core_copy(i).start()
        own_copy(i).start()
    sq[...] = jnp.zeros_like(sq)

    def advance(i, step):
        if step == 0:
            core_copy(i).wait_recv()
            own_copy(i).wait()
        if step < 4:
            for half in range(2):
                if step:
                    rs_copy(i, half, step).wait_recv()
                rs_step(i, half, step + 1)
        elif step == 4:
            for half in range(2):
                rs_copy(i, half, 4).wait_recv()
                finish(i, half)
                ag_copy(i, half, 4).start()
                ag_own(i, half).start()
        elif step < 8:
            for half in range(2):
                if step == 5:
                    ag_own(i, half).wait()
                ag_copy(i, half, 9 - step).wait_recv()
                ag_copy(i, half, 8 - step).start()
        elif step == 8:
            for half in range(2):
                ag_copy(i, half, 1).wait_recv()
            ag_core(i).start()
        else:
            ag_core(i).wait_recv()

    def sq_copy(away):
        to = lax.rem(me + away, n)
        return pltpu.make_async_remote_copy(
            sq, sq_out.at[me], sq_send.at[away], sq_recv.at[away], device_id={"dp": to}, device_id_type=MESH
        )

    for t in range(k + 9):
        for step in range(10):
            i = t - step
            if 0 <= i < k:
                advance(i, step)
                if step == 4 and i == k - 1:
                    sq_out[me] = sq[...]

                    @pl.loop(1, n)
                    def _(away):
                        sq_copy(away).start()

    @pl.loop(1, n)
    def _(away):
        sq_copy(away).wait()

    for i in range(k):
        core_copy(i).wait_send()
        ag_core(i).wait_send()
        for half in range(2):
            for stage in range(1, 5):
                rs_copy(i, half, stage).wait_send()
                ag_copy(i, half, stage).wait_send()


def all_reduce(grads, n):
    shapes, k = [g.shape for g in grads], len(grads)
    vmem = lambda rows, columns: pltpu.VMEM((rows, columns), jnp.bfloat16)
    scratch = [vmem(r // 2, c) for r, c in shapes]
    for r, c in shapes:
        scratch += [vmem(r >> (stage + 1), c) for stage in range(5)]
    scratch += [vmem(r // 32, c) for r, c in shapes]
    scratch += [pltpu.VMEM((16, 128), jnp.float32)]
    dma = pltpu.SemaphoreType.DMA
    scratch += [dma((k,)), dma((k, 2, 5)), dma((k, 2, 5)), dma((k, 2)), dma((k, 2, 5)), dma((k, 2, 5)), dma((n,)), dma((n,))]
    return pl.pallas_call(
        functools.partial(all_reduce_kernel, shapes, n),
        out_shape=[jax.ShapeDtypeStruct(g.shape, jnp.bfloat16) for g in grads]
        + [jax.ShapeDtypeStruct((n, 16, 128), jnp.float32)],
        in_specs=[pl.BlockSpec(memory_space=pl.ANY)] * k,
        out_specs=[pl.BlockSpec(memory_space=pl.ANY)] * k + [pl.BlockSpec(memory_space=pltpu.VMEM)],
        scratch_shapes=scratch,
        compiler_params=pltpu.CompilerParams(has_side_effects=True, vmem_limit_bytes=LIMIT),
        cost_estimate=pl.CostEstimate(flops=10**9, bytes_accessed=10**8, transcendentals=0),
        name="all_reduce",
    )(*grads)


def adamw_kernel(first, factor_ref, g0_ref, g1_ref, w_ref, m_ref, v_ref, w_out, m_out, v_out):
    factor = factor_ref[0, 0]

    def update(g_ref):
        g = g_ref[...].astype(jnp.float32) * factor
        m = 0.9 * m_ref[0] + 0.1 * g
        v = 0.95 * v_ref[0] + 0.05 * g * g
        w = w_ref[0].astype(jnp.float32)
        step = m * lax.rsqrt(v + 1e-8) + 0.1 * w
        w_out[0] = (w - 0.02 * step).astype(jnp.bfloat16)
        m_out[0] = m
        v_out[0] = v

    number = pl.program_id(0)

    @pl.when(number == 0)
    def _():
        update(g0_ref)

    @pl.when(number == 1)
    def _():
        update(g1_ref)


def adamw(factor, g0, g1, w, m, v, rows):
    layers, r, c = w.shape
    blocks = r // rows
    whole = pl.BlockSpec((1, rows, c), lambda number, i: (number, i, 0))
    in0 = pl.BlockSpec((rows, c), lambda number, i: (jnp.where(number == 0, i, blocks - 1), 0))
    in1 = pl.BlockSpec((rows, c), lambda number, i: (jnp.where(number == 1, i, 0), 0))
    return pl.pallas_call(
        functools.partial(adamw_kernel, 0),
        grid=(layers, blocks),
        out_shape=[jax.ShapeDtypeStruct(a.shape, a.dtype) for a in (w, m, v)],
        in_specs=[pl.BlockSpec((1, 1), lambda number, i: (0, 0), memory_space=pltpu.SMEM), in0, in1, whole, whole, whole],
        out_specs=[whole] * 3,
        compiler_params=pltpu.CompilerParams(vmem_limit_bytes=LIMIT, dimension_semantics=("arbitrary", "arbitrary")),
        cost_estimate=pl.CostEstimate(flops=20 * w.size, bytes_accessed=22 * w.size, transcendentals=w.size),
        name="adamw",
    )(factor, g0, g1, w, m, v)


def solution(mesh):
    n = mesh.shape["dp"]

    def step(x, dy, *arrays):
        weights, m, v = (arrays[i : i + 3] for i in (0, 3, 6))
        layers = weights[0].shape[0]
        h, kept = x[0], []
        for number in range(layers):
            kept.append(h)
            h = layer(h, {name: w[number] for name, w in zip(NAMES, weights, strict=True)})
        by_h, terms = dy[0], [None] * layers
        for number in reversed(range(layers)):
            _, back = jax.vjp(lambda w, h: layer(h, w), {name: w[number] for name, w in zip(NAMES, weights, strict=True)}, kept[number])
            by_w, by_h = back(by_h)
            terms[number] = [by_w[name] for name in NAMES]
        *summed, squares = all_reduce(terms[1] + terms[0], n)
        total = jnp.sum(squares)
        factor = jnp.minimum(1.0, 0.5 * lax.rsqrt(total / sum(w.size for w in weights) + 1e-30)).reshape(1, 1)
        pairs = zip(summed[3:], summed[:3], strict=True)
        new = [
            adamw(factor, *pair, w, m, v, rows)
            for pair, w, m, v, rows in zip(pairs, weights, m, v, (128, 128, 320), strict=True)
        ]
        return tuple(one[which] for which in range(3) for one in new)

    return jax.shard_map(
        step,
        mesh=mesh,
        in_specs=(P(("rep", "dp"), None, None),) * 2 + (P(None, None, None),) * 9,
        out_specs=(P("rep", None, None),) * 9,
        check_vma=False,
    )
```

time: 951 us -> 730 us (0.77)
  waiting for transfers between devices: 469 us -> 0 us
  Pallas kernels: 0 us -> 403 us
  other arithmetic: 143 us -> 7.9 us
  between operations: 16.6 us -> 1.99 us
    psum x1 -> x0, waiting for transfers between devices: 469 us -> none  [step(): summed[number] = [lax.psum(by_w[name], 'dp') for name in NAMES]]
    pallas_call x0 -> x4, Pallas kernels: none -> 403 us  [the longest x1 276 us: all_reduce(): pl.pallas_call(functools.partial(all_reduce_kernel, shapes, n), out_shape...]
    convert_element_type x2 -> x0, other arithmetic: 113 us -> none  [adamw(): return ((w - 0.02 * step).astype(jnp.bfloat16), m, v)]
    reduce_sum x3 -> x1, other arithmetic: 24 us -> 1.62 us  [step(): total = jnp.sum(squares)]
  transfers between devices with their start and end apart: 1 -> 0, of which waited for: 1 -> 0; matrix products, arithmetic and copies ran while one was open for 0% -> 0% of each run, Pallas kernels for 0% -> 0%
where the time goes in v1:
time: 730 us; the launch traced here: 722 us
  Pallas kernels  403 us (55%)
  matrix products  296 us (41%)
  local copies, waits for them, and re-layouts  13.2 us (2%)
  other arithmetic  7.9 us (1%)
    pallas_call x1, Pallas kernels, all_reduce(): pl.pallas_call(functools.partial(all_reduce_kernel, shapes, n), out_shape...  276 us
    pallas_call x3, Pallas kernels, adamw(): pl.pallas_call(functools.partial(adamw_kernel, 0), grid=(layers, blocks),...  127 us
    dot_general x5, matrix products, layer(): up = jnp.dot(a, w['w_up'], preferred_element_type=jnp.float32)  106 us
    dot_general x5, matrix products, layer(): gate = jnp.dot(a, w['w_gate'], preferred_element_type=jnp.float32)  104 us
    dot_general x5, matrix products, matmul(): jnp.dot(a, w, preferred_element_type=jnp.float32).astype(jnp.bfloat16)  86.2 us

profile of v1, /device:TPU:25, one launch (start us, length us, event | category | flops | bytes accessed | tf_op | source)
XLA Modules:
  0.0 721.7 jit_solution(4212881536963553251)
XLA Ops:
  0.6 6.4 copy.20
  7.1 3.1 fusion.15
  10.2 0.0 slice-start.3
  10.2 6.7 copy.21
  16.9 16.9 %convolution_convert_fusion.1 = bf16[2048,2560]{1,0:T(8,128)(2,1)} fusion(bf16[2,2560,1024]{2,1,0:T(8,128)(2,1)} %w_ref.5, bf16[1,2048,1024]{2,1,0:T(8,128)(2,1)} %param.12), kind=kOutput, calls=%fused_computation.27 | convolution fusion | flops 10742661120 | bytes 19922944 | tf_op jit(solution)/shard_map/transpose(jvp())/dot_general | solution.py:18
  33.8 0.0 slice-done.4
  33.8 14.1 %fusion.41 = f32[2048,2560]{1,0:T(8,128)} fusion(bf16[2,1024,2560]{2,1,0:T(8,128)(2,1)S(1)} %bitcast.66, bf16[1,2048,1024]{2,1,0:T(8,128)(2,1)S(1)} %copy-done.3, f32[2048]{0:T(1024)S(1)} %add_rsqrt_fusion), kind=kOutput, calls=%fused_computation.60 | convolution fusion | flops 10743709696 | bytes 30416896 | tf_op jit(solution)/shard_map/dot_general | solution.py:29
  47.9 26.7 %multiply_convert_fusion.1 = (bf16[2048,2560]{1,0:T(8,128)(2,1)}, f32[2048,2560]{1,0:T(8,128)}) fusion(f32[2048,2560]{1,0:T(8,128)} %fusion.41, bf16[2,1024,2560]{2,1,0:T(8,128)(2,1)} %w_ref.4, bf16[1,2048,1024]{2,1,0:T(8,128)(2,1)} %param.11, f32[2048]{0:T(1024)S(1)} %add_rsqrt_fusion), kind=kOutput, calls=%fused_computation.17 | convolution fusion | flops 10775166976 | bytes 61874176 | tf_op jit(solution)/shard_map/dot_general | solution.py:30
  74.7 17.9 %fusion.19 = (f32[2048]{0:T(1024)S(1)}, bf16[2048,1024]{0,1:T(8,128)(2,1)}) fusion(bf16[2048,2560]{1,0:T(8,128)(2,1)} %get-tuple-element.41, bf16[2,2560,1024]{2,1,0:T(8,128)(2,1)} %w_ref.5, bf16[1,2048,1024]{1,2,0:T(8,128)(2,1)S(1)} %copy-done.1), kind=kOutput, calls=%fused_computation.37 | convolution fusion | flops 10747901952 | bytes 24125440 | tf_op jit(solution)/shard_map/dot_general | solution.py:18
  92.6 18.5 %fusion.33 = f32[2048,2560]{1,0:T(8,128)} fusion(bf16[2,1024,2560]{2,1,0:T(8,128)(2,1)} %w_ref.4, bf16[2048,1024]{0,1:T(8,128)(2,1)} %get-tuple-element.44, f32[2048]{0:T(1024)S(1)} %fusion.69), kind=kOutput, calls=%fused_computation.52 | convolution fusion | flops 10743709696 | bytes 30416896 | tf_op jit(solution)/shard_map/jvp()/dot_general | solution.py:30
  111.1 0.0 copy-done.4
  111.1 32.1 %fusion.2 = (bf16[2048,2560]{1,0:T(8,128)(2,1)}, f32[2048,2560]{1,0:T(8,128)}) fusion(f32[2048,2560]{1,0:T(8,128)} %fusion.33, bf16[2048,2560]{1,0:T(8,128)(2,1)} %convolution_convert_fusion.1, bf16[2,1024,2560]{2,1,0:T(8,128)(2,1)} %w_ref.3, bf16[2048,1024]{0,1:T(8,128)(2,1)} %get-tuple-element.44, f32[2048]{0:T(1024)S(1)} %fusion.69), kind=kOutput, calls=%fused_computation.8 | convolution fusion | flops 10806624256 | bytes 72359936 | tf_op jit(solution)/shard_map/jvp()/dot_general | solution.py:29
  143.2 22.1 %fusion.22.refs_2_ = bf16[2560,1024]{1,0:T(8,128)(2,1)} fusion(f32[2048,2560]{1,0:T(8,128)} %fusion.33, bf16[1,2048,1024]{2,1,0:T(8,128)(2,1)} %param.12, f32[2048,2560]{1,0:T(8,128)} %get-tuple-element.46), kind=kOutput, calls=%fused_computation.41 | convolution fusion | flops 10771496960 | bytes 51380224 | tf_op jit(solution)/shard_map/transpose(jvp())/dot_general | solution.py:18
  165.3 19.8 %fusion.11 = bf16[2048,1024]{0,1:T(8,128)(2,1)} fusion(bf16[2048,2560]{1,0:T(8,128)(2,1)} %convolution_convert_fusion.1, bf16[2,1024,2560]{2,1,0:T(8,128)(2,1)} %w_ref.4, f32[2048,2560]{1,0:T(8,128)} %get-tuple-element.46), kind=kOutput, calls=%fused_computation.24 | convolution fusion | flops 10768875520 | bytes 40894464 | tf_op jit(solution)/shard_map/transpose(jvp())/dot_general | solution.py:30
  185.2 20.3 %fusion.23.refs_1_ = bf16[1024,2560]{1,0:T(8,128)(2,1)} fusion(bf16[2048,2560]{1,0:T(8,128)(2,1)} %convolution_convert_fusion.1, bf16[2048,1024]{0,1:T(8,128)(2,1)} %get-tuple-element.44, f32[2048]{0:T(1024)S(1)} %fusion.69, f32[2048,2560]{1,0:T(8,128)} %get-tuple-element.46), kind=kOutput, calls=%fused_computation.42 | convolution fusion | flops 10777788416 | bytes 40902656 | tf_op jit(solution)/shard_map/transpose(jvp())/dot_general | solution.py:30
  205.5 17.5 %fusion.21 = (f32[2048]{0:T(1024)S(1)}, bf16[2048,1024]{0,1:T(8,128)(2,1)S(1)}) fusion(bf16[2048,1024]{0,1:T(8,128)(2,1)} %get-tuple-element.44, bf16[2048,1024]{0,1:T(8,128)(2,1)} %fusion.11, bf16[2048,2560]{1,0:T(8,128)(2,1)} %get-tuple-element.45, bf16[2,1024,2560]{2,1,0:T(8,128)(2,1)} %w_ref.3), kind=kOutput, calls=%fused_computation.39 | convolution fusion | flops 10747901952 | bytes 28319744 | tf_op jit(solution)/shard_map/transpose(jvp())/dot_general | solution.py:29
  223.0 15.5 %convolution_convert_fusion.3.refs_0_ = bf16[1024,2560]{1,0:T(8,128)(2,1)} fusion(bf16[2048,2560]{1,0:T(8,128)(2,1)} %get-tuple-element.45, bf16[2048,1024]{0,1:T(8,128)(2,1)S(1)} %copy-done.2, f32[2048]{0:T(1024)S(1)} %fusion.69), kind=kOutput, calls=%fused_computation.46 | convolution fusion | flops 10743709696 | bytes 19931136 | tf_op jit(solution)/shard_map/transpose(jvp())/dot_general | solution.py:29
  238.6 0.0 slice-start
  238.6 3.2 fusion.53
  241.8 0.0 slice-start.1
  241.8 0.0 slice-start.2
  241.8 15.5 %convolution_convert_fusion.2.refs_5_ = bf16[2560,1024]{1,0:T(8,128)(2,1)} fusion(bf16[2048,2560]{1,0:T(8,128)(2,1)} %get-tuple-element.41, bf16[2048,1024]{0,1:T(8,128)(2,1)S(1)} %fusion.53), kind=kOutput, calls=%fused_computation.45 | convolution fusion | flops 10740039680 | bytes 19922944 | tf_op jit(solution)/shard_map/transpose(jvp())/dot_general | solution.py:18
  257.3 0.0 copy-start.7
  257.3 13.7 %convolution_convert_fusion = bf16[2048,2560]{1,0:T(8,128)(2,1)} fusion(bf16[2048,1024]{0,1:T(8,128)(2,1)S(1)} %fusion.53, bf16[2,2560,1024]{2,1,0:T(8,128)(2,1)S(1)} %bitcast.64), kind=kOutput, calls=%fused_computation.26 | convolution fusion | flops 10742661120 | bytes 19922944 | tf_op jit(solution)/shard_map/transpose(jvp())/dot_general | solution.py:18
  271.1 0.0 copy-done.7
  271.1 24.8 %fusion.24.refs_3_ = bf16[1024,2560]{1,0:T(8,128)(2,1)} fusion(f32[2048,2560]{1,0:T(8,128)} %fusion.41, f32[2048,2560]{1,0:T(8,128)} %get-tuple-element.42, bf16[2048,2560]{1,0:T(8,128)(2,1)} %convolution_convert_fusion, bf16[1,2048,1024]{1,2,0:T(8,128)(2,1)} %copy.20, f32[2048]{0:T(1024)S(1)} %copy-done.7), kind=kOutput, calls=%fused_computation.43 | convolution fusion | flops 10804002816 | bytes 61874176 | tf_op jit(solution)/shard_map/transpose(jvp())/dot_general | solution.py:29
  295.9 20.2 %fusion.27.refs_4_ = bf16[1024,2560]{1,0:T(8,128)(2,1)} fusion(bf16[2048,2560]{1,0:T(8,128)(2,1)} %convolution_convert_fusion, bf16[1,2048,1024]{1,2,0:T(8,128)(2,1)} %copy.20, f32[2048]{0:T(1024)S(1)} %copy-done.7, f32[2048,2560]{1,0:T(8,128)} %fusion.41), kind=kOutput, calls=%fused_computation.44 | convolution fusion | flops 10777788416 | bytes 40902656 | tf_op jit(solution)/shard_map/transpose(jvp())/dot_general | solution.py:30
  316.1 275.9 %all_reduce.1 = (bf16[1024,2560]{1,0:T(8,128)(2,1)}, bf16[1024,2560]{1,0:T(8,128)(2,1)}, bf16[2560,1024]{1,0:T(8,128)(2,1)}, bf16[1024,2560]{1,0:T(8,128)(2,1)},...) custom-call(bf16[1024,2560]{1,0:T(8,128)(2,1)} %convolution_convert_fusion.3.refs_0_, ...), custom_call_target="tpu_custom_call" | custom-call | flops 1000000000 | bytes 100000000 | tf_op jit(solution)/shard_map/all_reduce/pallas_call | solution.py:221
  592.0 1.6 reduce_sum.41
  594.3 42.3 %adamw.5 = (bf16[2,2560,1024]{2,1,0:T(8,128)(2,1)}, f32[2,2560,1024]{2,1,0:T(8,128)}, f32[2,2560,1024]{2,1,0:T(8,128)}) custom-call(f32[1,1]{1,0:T(1,128)} %bitcast.9.factor_ref, bf16[2560,1024]{1,0:T(8,128)(2,1)} %get-tuple-element.32.g0_ref, bf16[2560,1024]{1,0:T(8,128)(2,1)} %get-tuple-element.33.g1_ref, bf16[2,2560,1024]{2,1,0:T(8,128)(2,1)} %w_ref.5, ...), custom_call_target="tpu_custom_call" | custom-call | flops 104857600 | bytes 115343360 | tf_op jit(solution)/shard_map/adamw/pallas_call | solution.py:264
  636.6 42.3 %adamw.4 = (bf16[2,1024,2560]{2,1,0:T(8,128)(2,1)}, f32[2,1024,2560]{2,1,0:T(8,128)}, f32[2,1024,2560]{2,1,0:T(8,128)}) custom-call(f32[1,1]{1,0:T(1,128)} %bitcast.9.factor_ref, bf16[1024,2560]{1,0:T(8,128)(2,1)} %get-tuple-element.29.g0_ref, bf16[1024,2560]{1,0:T(8,128)(2,1)} %get-tuple-element.30.g1_ref, bf16[2,1024,2560]{2,1,0:T(8,128)(2,1)} %w_ref.4, ...), custom_call_target="tpu_custom_call" | custom-call | flops 104857600 | bytes 115343360 | tf_op jit(solution)/shard_map/adamw/pallas_call | solution.py:264
  678.9 42.3 %adamw.3 = (bf16[2,1024,2560]{2,1,0:T(8,128)(2,1)}, f32[2,1024,2560]{2,1,0:T(8,128)}, f32[2,1024,2560]{2,1,0:T(8,128)}) custom-call(f32[1,1]{1,0:T(1,128)} %bitcast.9.factor_ref, bf16[1024,2560]{1,0:T(8,128)(2,1)} %get-tuple-element.26.g0_ref, bf16[1024,2560]{1,0:T(8,128)(2,1)} %get-tuple-element.27.g1_ref, bf16[2,1024,2560]{2,1,0:T(8,128)(2,1)} %w_ref.3, ...), custom_call_target="tpu_custom_call" | custom-call | flops 104857600 | bytes 115343360 | tf_op jit(solution)/shard_map/adamw/pallas_call | solution.py:264
  (25 shorter events, 0.1 us)
Async XLA Ops:
  10.2 37.8 %copy-start.6 = (f32[2048]{0:T(1024)}, f32[2048]{0:T(1024)S(1)}, u32[]{:S(2)}) copy-start(f32[2048]{0:T(1024)S(1)} %add_rsqrt_fusion) | copy-start | bytes 24580
  10.2 23.6 %slice-start.3 = ((s8[10485760]{0:T(1024)(128)(4,1)}), s8[2097152]{0:T(1024)(128)(4,1)S(1)}, s32[]{:S(2)}) async-start(s8[10485760]{0:T(1024)(128)(4,1)} %bitcast.65), calls=%async_computation.3 | async-start | bytes 4194304
  16.9 16.9 %slice-start.4 = ((s8[10485760]{0:T(1024)(128)(4,1)}), s8[4194304]{0:T(1024)(128)(4,1)S(1)}, s32[]{:S(2)}) async-start(s8[10485760]{0:T(1024)(128)(4,1)} %bitcast.65), calls=%async_computation.4 | async-start | bytes 8388608
  16.9 16.9 %slice-start.5 = ((s8[10485760]{0:T(1024)(128)(4,1)}), s8[4194304]{0:T(1024)(128)(4,1)S(1)}, s32[]{:S(2)}) async-start(s8[10485760]{0:T(1024)(128)(4,1)} %bitcast.65), calls=%async_computation.5 | async-start | bytes 8388608
  16.9 16.9 %copy-start.3 = (bf16[1,2048,1024]{2,1,0:T(8,128)(2,1)S(1)}, bf16[1,2048,1024]{2,1,0:T(8,128)(2,1)}, u32[]{:S(2)}) copy-start(bf16[1,2048,1024]{2,1,0:T(8,128)(2,1)} %param.11) | copy-start | bytes 12582916
  47.9 26.7 %copy-start.1 = (bf16[1,2048,1024]{1,2,0:T(8,128)(2,1)S(1)}, bf16[1,2048,1024]{1,2,0:T(8,128)(2,1)}, u32[]{:S(2)}) copy-start(bf16[1,2048,1024]{1,2,0:T(8,128)(2,1)} %copy.20) | copy-start | bytes 12582916
  92.6 18.5 %copy-start.4 = (f32[2048]{0:T(1024)}, f32[2048]{0:T(1024)S(1)}, u32[]{:S(2)}) copy-start(f32[2048]{0:T(1024)S(1)} %get-tuple-element.43) | copy-start | bytes 24580
  205.5 17.5 %copy-start.2 = (bf16[2048,1024]{0,1:T(8,128)(2,1)S(1)}, bf16[2048,1024]{0,1:T(8,128)(2,1)}, u32[]{:S(2)}) copy-start(bf16[2048,1024]{0,1:T(8,128)(2,1)} %get-tuple-element.44) | copy-start | bytes 12582916
  223.0 15.5 %copy-start.5 = (f32[2048]{0:T(1024)S(1)}, f32[2048]{0:T(1024)}, u32[]{:S(2)}) copy-start(f32[2048]{0:T(1024)} %copy-done.4) | copy-start | bytes 24580
  223.0 15.5 %copy-start = (bf16[1,2048,1024]{1,2,0:T(8,128)(2,1)S(1)}, bf16[1,2048,1024]{1,2,0:T(8,128)(2,1)}, u32[]{:S(2)}) copy-start(bf16[1,2048,1024]{1,2,0:T(8,128)(2,1)} %copy.21) | copy-start | bytes 12582916
  238.6 18.7 %slice-start = ((s8[10485760]{0:T(1024)(128)(4,1)}), s8[4194304]{0:T(1024)(128)(4,1)S(1)}, s32[]{:S(2)}) async-start(s8[10485760]{0:T(1024)(128)(4,1)} %bitcast.63), calls=%async_computation | async-start | bytes 8388608
  241.8 15.5 %slice-start.1 = ((s8[10485760]{0:T(1024)(128)(4,1)}), s8[4194304]{0:T(1024)(128)(4,1)S(1)}, s32[]{:S(2)}) async-start(s8[10485760]{0:T(1024)(128)(4,1)} %bitcast.63), calls=%async_computation.1 | async-start | bytes 8388608
  241.8 15.5 %slice-start.2 = ((s8[10485760]{0:T(1024)(128)(4,1)}), s8[2097152]{0:T(1024)(128)(4,1)S(1)}, s32[]{:S(2)}) async-start(s8[10485760]{0:T(1024)(128)(4,1)} %bitcast.63), calls=%async_computation.2 | async-start | bytes 4194304
  257.3 13.8 %copy-start.7 = (f32[2048]{0:T(1024)S(1)}, f32[2048]{0:T(1024)}, u32[]{:S(2)}) copy-start(f32[2048]{0:T(1024)} %copy-done.6) | copy-start | bytes 24580

commit v2 on v1

v2 whole, which is shorter than its diff:
```python
import functools

import jax
import jax.numpy as jnp
from jax import lax
from jax.experimental import pallas as pl
from jax.experimental.pallas import tpu as pltpu
from jax.sharding import PartitionSpec as P

MESH = pl.DeviceIdType.MESH
LIMIT = 66_000_000
CORE, Z1, Z2, Y, X = 1, 2, 4, 8, 16
ORDERS = ((X, Z1, Y, Z2), (Y, Z1, X, Z2))


def f32dot(a, w, over=0):
    return lax.dot_general(a, w, (((1,), (over,)), ((), ())), preferred_element_type=jnp.float32)


def normed(h):
    wide = h.astype(jnp.float32)
    scale = lax.rsqrt(jnp.mean(wide**2, -1, keepdims=True) + 1e-6)
    return (wide * scale).astype(jnp.bfloat16), scale


def bit_of(me, stride):
    return lax.rem(lax.div(me, stride), 2)


def other(me, stride):
    return me + stride * (1 - 2 * bit_of(me, stride))


ROWS, COLS, TOKENS, TILE = 1024, 2560, 2048, 512
TILES = COLS // TILE
HALF, WIDTH = ROWS // 2, COLS // 2


def gradients_kernel(which, n, *refs):
    k = len(which)
    count = max(which) + 1
    lhs, rhs, outs, sq_out = refs[:count], refs[count : count + k], refs[count + k : count + 2 * k], refs[count + 2 * k]
    refs = refs[count + 2 * k + 1 :]
    own, landed, refs = refs[:k], [refs[k + 5 * i : k + 5 * i + 5] for i in range(k)], refs[6 * k :]
    final, (sq, raw, turned, right, away) = refs[:k], refs[k : k + 5]
    raw_sem, right_sem, core_send, core_recv, send_sem, recv_sem, ag_local, ag_send, ag_recv, sq_send, sq_recv = refs[k + 5 :]
    me = lax.axis_index("dp")
    core = bit_of(me, CORE)

    def remote(src, dst, send, recv, stride):
        return pltpu.make_async_remote_copy(src, dst, send, recv, device_id={"dp": other(me, stride)}, device_id_type=MESH)

    def columns(half):
        return pl.ds(half * WIDTH, WIDTH)

    def starts(half):
        size, at = HALF, 0
        found = [at]
        for stride in ORDERS[half]:
            size //= 2
            at = at + bit_of(me, stride) * size
            found.append(at)
        return found

    def raw_copy(index):
        return pltpu.make_async_copy(lhs[index], raw, raw_sem)

    def right_copy(i, j):
        slot = lax.rem(i * TILES + j, 2)
        cols = pl.ds(pl.multiple_of(j * TILE, TILE), TILE)
        return pltpu.make_async_copy(rhs[i].at[:, cols], right.at[slot], right_sem.at[slot])

    def core_copy(i, j):
        cols = pl.ds(pl.multiple_of(j * TILE, TILE), TILE)
        return remote(away.at[lax.rem(j, 2)], landed[i][0].at[:, cols], core_send.at[i, j], core_recv.at[i, j], CORE)

    def rs_copy(i, half, stage):
        stride = ORDERS[half][stage - 1]
        size = ROWS >> (stage + 1)
        at = starts(half)[stage - 1] + (1 - bit_of(me, stride)) * size
        cols = columns(half)
        return remote(
            own[i].at[pl.ds(pl.multiple_of(at, 16), size), cols],
            landed[i][stage].at[:, cols],
            send_sem.at[i, half, stage],
            recv_sem.at[i, half, stage],
            stride,
        )

    def summed(i, half, stage, at, row):
        cols, found = columns(half), starts(half)
        place = lambda start: pl.ds(pl.multiple_of(at - start + row, 16), 16)
        total = own[i][place(0), cols].astype(jnp.float32)
        for s in range(stage + 1):
            total += landed[i][s][place(found[s]), cols].astype(jnp.float32)
        return total

    def rs_step(i, half, stage):
        stride = ORDERS[half][stage - 1]
        size = ROWS >> (stage + 1)
        at = starts(half)[stage - 1] + (1 - bit_of(me, stride)) * size

        @pl.loop(0, size // 16)
        def _(block):
            row = block * 16
            total = summed(i, half, stage - 1, at, row)
            own[i][pl.ds(pl.multiple_of(at + row, 16), 16), columns(half)] = total.astype(jnp.bfloat16)

        rs_copy(i, half, stage).start()

    def finish(i, half):
        at = starts(half)[4]

        @pl.loop(0, ROWS // 32 // 16)
        def _(block):
            row = block * 16
            total = summed(i, half, 4, at, row).astype(jnp.bfloat16)
            final[i][pl.ds(pl.multiple_of(row, 16), 16), columns(half)] = total
            wide = total.astype(jnp.float32)
            wide = wide * wide
            part = wide[:, :128]
            for j in range(1, WIDTH // 128):
                part += wide[:, j * 128 : (j + 1) * 128]
            sq[...] += part

    def region(half, stage):
        at = core * HALF + starts(half)[stage]
        return pl.ds(pl.multiple_of(at, 16), ROWS >> (stage + 1)), columns(half)

    def ag_copy(i, half, stage):
        rows, cols = region(half, stage)
        src = final[i].at[:, cols] if stage == 4 else outs[i].at[rows, cols]
        return remote(
            src, outs[i].at[rows, cols], ag_send.at[i, half, stage], ag_recv.at[i, half, stage], ORDERS[half][stage - 1]
        )

    def ag_own(i, half):
        rows, cols = region(half, 4)
        return pltpu.make_async_copy(final[i].at[:, cols], outs[i].at[rows, cols], ag_local.at[i, half])

    def ag_core(i):
        mine = pl.ds(pl.multiple_of(core * HALF, 16), HALF)
        return remote(outs[i].at[mine, :], outs[i].at[mine, :], ag_send.at[i, 0, 0], ag_recv.at[i, 0, 0], CORE)

    def advance(i, step):
        if step == 0:
            for j in range(TILES):
                core_copy(i, j).wait_recv()
        if step < 4:
            for half in range(2):
                if step:
                    rs_copy(i, half, step).wait_recv()
                rs_step(i, half, step + 1)
        elif step == 4:
            for half in range(2):
                rs_copy(i, half, 4).wait_recv()
                finish(i, half)
                ag_copy(i, half, 4).start()
                ag_own(i, half).start()
        elif step < 8:
            for half in range(2):
                if step == 5:
                    ag_own(i, half).wait()
                ag_copy(i, half, 9 - step).wait_recv()
                ag_copy(i, half, 8 - step).start()
        elif step == 8:
            for half in range(2):
                ag_copy(i, half, 1).wait_recv()
            ag_core(i).start()
        else:
            ag_core(i).wait_recv()

    def sq_copy(hops):
        to = lax.rem(me + hops, n)
        return pltpu.make_async_remote_copy(
            sq, sq_out.at[me], sq_send.at[hops], sq_recv.at[hops], device_id={"dp": to}, device_id_type=MESH
        )

    def turn():
        @pl.loop(0, TOKENS // 128)
        def _(block):
            at = pl.ds(pl.multiple_of(block * 128, 128), 128)
            turned[:, at] = raw[at, :].T

    def product(i, j):
        slot = lax.rem(i * TILES + j, 2)
        right_copy(i, j).wait()

        @pl.when(j + 1 < TILES)
        def _():
            right_copy(i, j + 1).start()

        if i + 1 < k:

            @pl.when(j + 1 == TILES)
            def _():
                right_copy(i + 1, 0).start()

        half = lambda which: turned[pl.ds(pl.multiple_of(which * HALF, HALF), HALF), :]
        dot = lambda a: jnp.dot(a, right[slot], preferred_element_type=jnp.float32).astype(jnp.bfloat16)
        away[lax.rem(j, 2)] = dot(half(1 - core))
        core_copy(i, j).start()
        own[i][:, pl.ds(pl.multiple_of(j * TILE, TILE), TILE)] = dot(half(core))

        @pl.when(j >= 1)
        def _():
            core_copy(i, j - 1).wait_send()

    def due(t):
        return [(t - 1 - step, step) for step in range(10) if 0 <= t - 1 - step < k]

    raw_copy(which[0]).start()
    right_copy(0, 0).start()
    sq[...] = jnp.zeros_like(sq)
    for t in range(k):
        if t == 0 or which[t] != which[t - 1]:
            raw_copy(which[t]).wait()
            turn()
            if which[t] + 1 < count:
                raw_copy(which[t] + 1).start()

        @pl.loop(0, TILES)
        def _(j):
            product(t, j)
            for place in range(TILES):
                some = [(i, step) for i, step in due(t) if step // 2 == place]
                if some:

                    @pl.when(j == place)
                    def _():
                        for i, step in some:
                            advance(i, step)

        core_copy(t, TILES - 1).wait_send()

    for t in range(k, k + 10):
        for i, step in due(t):
            advance(i, step)
            if step == 4 and i == k - 1:
                sq_out[me] = sq[...]

                @pl.loop(1, n)
                def _(hops):
                    sq_copy(hops).start()

    @pl.loop(1, n)
    def _(hops):
        sq_copy(hops).wait()

    for i in range(k):
        ag_core(i).wait_send()
        for half in range(2):
            for stage in range(1, 5):
                rs_copy(i, half, stage).wait_send()
                ag_copy(i, half, stage).wait_send()


def gradients(lhs, rhs, which, n):
    k = len(which)
    vmem = lambda *shape: pltpu.VMEM(shape, jnp.bfloat16)
    scratch = [vmem(HALF, COLS)] * k + [vmem(ROWS >> (stage + 1), COLS) for stage in range(5)] * k + [vmem(ROWS // 32, COLS)] * k
    scratch += [pltpu.VMEM((16, 128), jnp.float32), vmem(TOKENS, ROWS), vmem(ROWS, TOKENS), vmem(2, TOKENS, TILE), vmem(2, HALF, TILE)]
    dma = pltpu.SemaphoreType.DMA
    scratch += [dma, dma((2,)), dma((k, TILES)), dma((k, TILES)), dma((k, 2, 5)), dma((k, 2, 5))]
    scratch += [dma((k, 2)), dma((k, 2, 5)), dma((k, 2, 5)), dma((n,)), dma((n,))]
    return pl.pallas_call(
        functools.partial(gradients_kernel, which, n),
        out_shape=[jax.ShapeDtypeStruct((ROWS, COLS), jnp.bfloat16)] * k + [jax.ShapeDtypeStruct((n, 16, 128), jnp.float32)],
        in_specs=[pl.BlockSpec(memory_space=pl.ANY)] * (len(lhs) + k),
        out_specs=[pl.BlockSpec(memory_space=pl.ANY)] * k + [pl.BlockSpec(memory_space=pltpu.VMEM)],
        scratch_shapes=scratch,
        compiler_params=pltpu.CompilerParams(has_side_effects=True, vmem_limit_bytes=LIMIT),
        cost_estimate=pl.CostEstimate(flops=2 * k * TOKENS * ROWS * COLS, bytes_accessed=10**8, transcendentals=0),
        name="gradients",
    )(*lhs, *rhs)


def adamw_kernel(turned, factor_ref, g0_ref, g1_ref, w_ref, m_ref, v_ref, w_out, m_out, v_out):
    factor = factor_ref[0, 0]

    rows = w_ref.shape[1]
    strip = 128 if turned else 16

    def update(g_ref):
        @pl.loop(0, rows // strip)
        def _(block):
            at = pl.ds(pl.multiple_of(block * strip, strip), strip)
            g = (g_ref[:, at].astype(jnp.float32).T if turned else g_ref[at, :].astype(jnp.float32)) * factor
            m = 0.9 * m_ref[0, at] + 0.1 * g
            v = 0.95 * v_ref[0, at] + 0.05 * g * g
            w = w_ref[0, at].astype(jnp.float32)
            step = m * lax.rsqrt(v + 1e-8) + 0.1 * w
            w_out[0, at] = (w - 0.02 * step).astype(jnp.bfloat16)
            m_out[0, at] = m
            v_out[0, at] = v

    number = pl.program_id(0)

    @pl.when(number == 0)
    def _():
        update(g0_ref)

    @pl.when(number == 1)
    def _():
        update(g1_ref)


def adamw(factor, g0, g1, w, m, v, rows, turned):
    layers, r, c = w.shape
    blocks = r // rows
    whole = pl.BlockSpec((1, rows, c), lambda number, i: (number, i, 0))
    shape = (c, rows) if turned else (rows, c)
    at = lambda i: (0, i) if turned else (i, 0)
    in0 = pl.BlockSpec(shape, lambda number, i: at(jnp.where(number == 0, i, blocks - 1)))
    in1 = pl.BlockSpec(shape, lambda number, i: at(jnp.where(number == 1, i, 0)))
    return pl.pallas_call(
        functools.partial(adamw_kernel, turned),
        grid=(layers, blocks),
        out_shape=[jax.ShapeDtypeStruct(a.shape, a.dtype) for a in (w, m, v)],
        in_specs=[pl.BlockSpec((1, 1), lambda number, i: (0, 0), memory_space=pltpu.SMEM), in0, in1, whole, whole, whole],
        out_specs=[whole] * 3,
        compiler_params=pltpu.CompilerParams(vmem_limit_bytes=LIMIT, dimension_semantics=("arbitrary", "arbitrary")),
        cost_estimate=pl.CostEstimate(flops=20 * w.size, bytes_accessed=22 * w.size, transcendentals=w.size),
        name="adamw",
    )(factor, g0, g1, w, m, v)


def solution(mesh):
    n = mesh.shape["dp"]

    def step(x, dy, *arrays):
        weights, m, v = (arrays[i : i + 3] for i in (0, 3, 6))
        layers = weights[0].shape[0]
        (w_gate, w_up, w_down), kept = weights, []
        h = x[0]
        for number in range(layers):
            a, scale = normed(h)
            gate, up = f32dot(a, w_gate[number]), f32dot(a, w_up[number])
            kept.append((h, a, scale, gate, up))
            if number + 1 < layers:
                h = h + f32dot((jax.nn.silu(gate) * up).astype(jnp.bfloat16), w_down[number]).astype(jnp.bfloat16)
        by_h, lhs, rhs = dy[0], [], []
        for number in reversed(range(layers)):
            h, a, scale, gate, up = kept[number]
            by_act = f32dot(by_h, w_down[number], 1).astype(jnp.bfloat16).astype(jnp.float32)
            sig = jax.nn.sigmoid(gate)
            silu = gate * sig
            act = (silu * up).astype(jnp.bfloat16)
            by_up = (by_act * silu).astype(jnp.bfloat16)
            by_gate = (by_act * up * (sig + silu * (1 - sig))).astype(jnp.bfloat16)
            lhs += [by_h, a]
            rhs += [act, by_gate, by_up]
            if number:
                by_a = f32dot(by_gate, w_gate[number], 1) + f32dot(by_up, w_up[number], 1)
                by_a, wide = by_a.astype(jnp.bfloat16).astype(jnp.float32), h.astype(jnp.float32)
                by_scale = jnp.sum(by_a * wide, -1, keepdims=True)
                by_wide = by_a * scale - wide * (scale * scale * scale * by_scale / h.shape[-1])
                by_h = by_h + by_wide.astype(jnp.bfloat16)
        down1, gate1, up1, down0, gate0, up0, squares = gradients(lhs, rhs, (0, 1, 1, 2, 3, 3), n)
        total = jnp.sum(squares)
        factor = jnp.minimum(1.0, 0.5 * lax.rsqrt(total / sum(w.size for w in weights) + 1e-30)).reshape(1, 1)
        pairs = ((gate0, gate1), (up0, up1), (down0, down1))
        new = [
            adamw(factor, *pair, w, m, v, rows, turned)
            for pair, w, m, v, rows, turned in zip(pairs, weights, m, v, (256, 256, 640), (False, False, True), strict=True)
        ]
        return tuple(one[which] for which in range(3) for one in new)

    return jax.shard_map(
        step,
        mesh=mesh,
        in_specs=(P(("rep", "dp"), None, None),) * 2 + (P(None, None, None),) * 9,
        out_specs=(P("rep", None, None),) * 9,
        check_vma=False,
    )
```

time: 730 us -> 638 us (0.87)
  matrix products: 296 us -> 199 us
  local copies, waits for them, and re-layouts: 13.2 us -> 2 us
  Pallas kernels: 403 us -> 413 us
    dot_general x15 -> x9, matrix products: 296 us -> 199 us  [f32dot(): lax.dot_general(a, w, (((1,), (over,)), ((), ())), preferred_element_type...]
    unnamed x30 -> x12, local copies, waits for them, and re-layouts: 13.2 us -> 2 us
    pallas_call x4, Pallas kernels: 403 us -> 413 us  [the longest x1 297 us: gradients(): pl.pallas_call(functools.partial(gradients_kernel, which, n), out_shape=[...]
where the time goes in v2:
time: 638 us; the launch traced here: 630 us
  Pallas kernels  413 us (65%)
  matrix products  199 us (31%)
  other arithmetic  13.6 us (2%)
    pallas_call x1, Pallas kernels, gradients(): pl.pallas_call(functools.partial(gradients_kernel, which, n), out_shape=[...  297 us
    dot_general x9, matrix products, f32dot(): lax.dot_general(a, w, (((1,), (over,)), ((), ())), preferred_element_type...  199 us
    pallas_call x3, Pallas kernels, adamw(): pl.pallas_call(functools.partial(adamw_kernel, turned), grid=(layers, blo...  117 us

profile of v2, /device:TPU:25, one launch (start us, length us, event | category | flops | bytes accessed | tf_op | source)
XLA Modules:
  0.0 629.9 jit_solution(5507853367262275512)
XLA Ops:
  0.6 0.0 slice-start
  0.7 3.2 fusion.8
  3.9 0.0 copy-start
  3.9 0.0 slice-start.1
  3.9 0.0 slice-start.2
  3.9 16.9 %convolution_convert_fusion.1 = bf16[2048,2560]{1,0:T(8,128)(2,1)} fusion(bf16[2,2560,1024]{2,1,0:T(8,128)(2,1)} %w_ref.5, bf16[1,2048,1024]{2,1,0:T(8,128)(2,1)} %param.12), kind=kOutput, calls=%fused_computation.21 | convolution fusion | flops 10742661120 | bytes 19922944 | tf_op jit(solution)/shard_map/dot_general | solution.py:17
  20.8 0.0 slice-done
  20.8 0.0 copy-done
  20.8 0.0 slice-done.1
  20.8 0.0 slice-done.2
  20.8 14.2 %fusion.29 = f32[2048,2560]{1,0:T(8,128)} fusion(bf16[2,1024,2560]{2,1,0:T(8,128)(2,1)S(1)} %bitcast.60, bf16[1,2048,1024]{2,1,0:T(8,128)(2,1)S(1)} %copy-done, f32[2048]{0:T(1024)S(1)} %add_rsqrt_fusion.1), kind=kOutput, calls=%fused_computation.48 | convolution fusion | flops 10743709696 | bytes 30416896 | tf_op jit(solution)/shard_map/dot_general | solution.py:17
  35.0 24.7 %multiply_convert_fusion.1 = (bf16[2048,2560]{1,0:T(8,128)(2,1)}, f32[2048,2560]{1,0:T(8,128)}) fusion(f32[2048,2560]{1,0:T(8,128)} %fusion.29, bf16[2,1024,2560]{2,1,0:T(8,128)(2,1)} %w_ref.4, bf16[1,2048,1024]{2,1,0:T(8,128)(2,1)S(1)} %copy-done, f32[2048]{0:T(1024)S(1)} %add_rsqrt_fusion.1), kind=kOutput, calls=%fused_computation.12 | convolution fusion | flops 10775166976 | bytes 61874176 | tf_op jit(solution)/shard_map/dot_general | solution.py:17
  59.7 0.0 copy-start.1
  59.7 16.6 %fusion.12 = (f32[2048]{0:T(1024)S(1)}, bf16[2048,1024]{1,0:T(8,128)(2,1)S(1)}) fusion(bf16[2048,2560]{1,0:T(8,128)(2,1)} %get-tuple-element.46.refs_7_, bf16[2,2560,1024]{2,1,0:T(8,128)(2,1)} %w_ref.5, bf16[1,2048,1024]{2,1,0:T(8,128)(2,1)} %param.11), kind=kOutput, calls=%fused_computation.29 | convolution fusion | flops 10747901952 | bytes 24125440 | tf_op jit(solution)/shard_map/dot_general | solution.py:17
  76.3 0.0 copy-done.1
  76.3 2.8 fusion.9
  79.1 0.0 copy-start.2
  79.1 2.0 copy-done.2
  81.1 17.2 %fusion.17 = f32[2048,2560]{1,0:T(8,128)} fusion(bf16[2048,1024]{1,0:T(8,128)(2,1)S(1)} %get-tuple-element.53.refs_1_, bf16[2,1024,2560]{2,1,0:T(8,128)(2,1)} %w_ref.3), kind=kOutput, calls=%fused_computation.36 | convolution fusion | flops 10737418240 | bytes 30408704 | tf_op jit(solution)/shard_map/dot_general | solution.py:17
  98.2 43.5 %multiply_convert_fusion = (bf16[2048,2560]{1,0:T(8,128)(2,1)}, bf16[2048,2560]{1,0:T(8,128)(2,1)}, bf16[2048,2560]{1,0:T(8,128)(2,1)}) fusion(f32[2048,2560]{1,0:T(8,128)} %fusion.17, bf16[2048,2560]{1,0:T(8,128)(2,1)} %convolution_convert_fusion.1, bf16[2048,1024]{1,0:T(8,128)(2,1)} %copy-done.2, bf16[2,1024,2560]{2,1,0:T(8,128)(2,1)} %w_ref.4), kind=kOutput, calls=%fused_computation.10 | convolution fusion | flops 10816061440 | bytes 72351744 | tf_op jit(solution)/shard_map/dot_general | solution.py:17
  141.8 16.6 %fusion.15 = f32[2048,1024]{1,0:T(8,128)} fusion(bf16[2048,2560]{1,0:T(8,128)(2,1)} %get-tuple-element.42.refs_5_, bf16[2,1024,2560]{2,1,0:T(8,128)(2,1)} %w_ref.3), kind=kOutput, calls=%fused_computation.34 | convolution fusion | flops 10737418240 | bytes 24117248 | tf_op jit(solution)/shard_map/dot_general | solution.py:17
  158.4 18.1 %fusion.14 = (f32[2048]{0:T(1024)S(1)}, bf16[2048,1024]{1,0:T(8,128)(2,1)}) fusion(bf16[2048,1024]{1,0:T(8,128)(2,1)S(1)} %get-tuple-element.49, f32[2048,1024]{1,0:T(8,128)} %fusion.15, bf16[2048,2560]{1,0:T(8,128)(2,1)} %get-tuple-element.43.refs_6_, bf16[2,1024,2560]{2,1,0:T(8,128)(2,1)} %w_ref.4), kind=kOutput, calls=%fused_computation.31 | convolution fusion | flops 10749999104 | bytes 32514048 | tf_op jit(solution)/shard_map/dot_general | solution.py:17
  176.5 5.9 fusion.41.refs_2_
  182.4 31.6 %fusion.5 = (bf16[2048,2560]{1,0:T(8,128)(2,1)}, bf16[2048,2560]{1,0:T(8,128)(2,1)}) fusion(f32[2048,2560]{1,0:T(8,128)} %fusion.29, f32[2048,2560]{1,0:T(8,128)} %get-tuple-element.47, bf16[2048,1024]{1,0:T(8,128)(2,1)} %fusion.41.refs_2_, bf16[2,2560,1024]{2,1,0:T(8,128)(2,1)} %w_ref.5), kind=kOutput, calls=%fused_computation.9 | convolution fusion | flops 10810818560 | bytes 72351744 | tf_op jit(solution)/shard_map/dot_general | solution.py:17
  214.0 296.6 %gradients.1 = (bf16[1024,2560]{1,0:T(8,128)(2,1)}, bf16[1024,2560]{1,0:T(8,128)(2,1)}, bf16[1024,2560]{1,0:T(8,128)(2,1)}, bf16[1024,2560]{1,0:T(8,128)(2,1)}, ...) custom-call(bf16[2048,1024]{1,0:T(8,128)(2,1)} %bitcast.61, ...), custom_call_target="tpu_custom_call" | custom-call | flops 64424509440 | bytes 100000000 | tf_op jit(solution)/shard_map/gradients/pallas_call | solution.py:266
  510.6 1.6 reduce_sum.39
  512.9 39.5 %adamw.5 = (bf16[2,2560,1024]{2,1,0:T(8,128)(2,1)}, f32[2,2560,1024]{2,1,0:T(8,128)}, f32[2,2560,1024]{2,1,0:T(8,128)}) custom-call(f32[1,1]{1,0:T(1,128)} %bitcast.9.factor_ref, bf16[1024,2560]{1,0:T(8,128)(2,1)} %get-tuple-element.32.g0_ref, bf16[1024,2560]{1,0:T(8,128)(2,1)} %get-tuple-element.33.g1_ref, bf16[2,2560,1024]{2,1,0:T(8,128)(2,1)} %w_ref.5, ...), custom_call_target="tpu_custom_call" | custom-call | flops 104857600 | bytes 115343360 | tf_op jit(solution)/shard_map/adamw/pallas_call | solution.py:316
  552.4 38.5 %adamw.4 = (bf16[2,1024,2560]{2,1,0:T(8,128)(2,1)}, f32[2,1024,2560]{2,1,0:T(8,128)}, f32[2,1024,2560]{2,1,0:T(8,128)}) custom-call(f32[1,1]{1,0:T(1,128)} %bitcast.9.factor_ref, bf16[1024,2560]{1,0:T(8,128)(2,1)} %get-tuple-element.29.g0_ref, bf16[1024,2560]{1,0:T(8,128)(2,1)} %get-tuple-element.30.g1_ref, bf16[2,1024,2560]{2,1,0:T(8,128)(2,1)} %w_ref.4, ...), custom_call_target="tpu_custom_call" | custom-call | flops 104857600 | bytes 115343360 | tf_op jit(solution)/shard_map/adamw/pallas_call | solution.py:316
  591.0 38.5 %adamw.3 = (bf16[2,1024,2560]{2,1,0:T(8,128)(2,1)}, f32[2,1024,2560]{2,1,0:T(8,128)}, f32[2,1024,2560]{2,1,0:T(8,128)}) custom-call(f32[1,1]{1,0:T(1,128)} %bitcast.9.factor_ref, bf16[1024,2560]{1,0:T(8,128)(2,1)} %get-tuple-element.26.g0_ref, bf16[1024,2560]{1,0:T(8,128)(2,1)} %get-tuple-element.27.g1_ref, bf16[2,1024,2560]{2,1,0:T(8,128)(2,1)} %w_ref.3, ...), custom_call_target="tpu_custom_call" | custom-call | flops 104857600 | bytes 115343360 | tf_op jit(solution)/shard_map/adamw/pallas_call | solution.py:316
  (4 shorter events, 0.0 us)
Async XLA Ops:
  0.6 20.2 %slice-start = ((s8[10485760]{0:T(1024)(128)(4,1)}), s8[4194304]{0:T(1024)(128)(4,1)S(1)}, s32[]{:S(2)}) async-start(s8[10485760]{0:T(1024)(128)(4,1)} %bitcast.59), calls=%async_computation | async-start | bytes 8388608
  3.9 16.9 %copy-start = (bf16[1,2048,1024]{2,1,0:T(8,128)(2,1)S(1)}, bf16[1,2048,1024]{2,1,0:T(8,128)(2,1)}, u32[]{:S(2)}) copy-start(bf16[1,2048,1024]{2,1,0:T(8,128)(2,1)} %param.11) | copy-start | bytes 12582916
  3.9 16.9 %slice-start.1 = ((s8[10485760]{0:T(1024)(128)(4,1)}), s8[4194304]{0:T(1024)(128)(4,1)S(1)}, s32[]{:S(2)}) async-start(s8[10485760]{0:T(1024)(128)(4,1)} %bitcast.59), calls=%async_computation.1 | async-start | bytes 8388608
  3.9 16.9 %slice-start.2 = ((s8[10485760]{0:T(1024)(128)(4,1)}), s8[2097152]{0:T(1024)(128)(4,1)S(1)}, s32[]{:S(2)}) async-start(s8[10485760]{0:T(1024)(128)(4,1)} %bitcast.59), calls=%async_computation.2 | async-start | bytes 4194304
  59.7 16.7 %copy-start.1 = (bf16[1,2048,1024]{2,1,0:T(8,128)(2,1)S(1)}, bf16[1,2048,1024]{2,1,0:T(8,128)(2,1)}, u32[]{:S(2)}) copy-start(bf16[1,2048,1024]{2,1,0:T(8,128)(2,1)} %param.11) | copy-start | bytes 12582916
  79.1 2.0 copy-start.2

commit v3 on v2

v3 whole, which is shorter than its diff:
```python
import functools

import jax
import jax.numpy as jnp
from jax import lax
from jax.experimental import pallas as pl
from jax.experimental.pallas import tpu as pltpu
from jax.sharding import PartitionSpec as P

MESH = pl.DeviceIdType.MESH
LIMIT = 66_000_000
CORE, Z1, Z2, Y, X = 1, 2, 4, 8, 16
ORDERS = ((X, Z1, Y, Z2), (Y, Z1, X, Z2))


def f32dot(a, w, over=0):
    return lax.dot_general(a, w, (((1,), (over,)), ((), ())), preferred_element_type=jnp.float32)


def scale_of(wide):
    return lax.rsqrt(jnp.mean(wide * wide, -1, keepdims=True) + 1e-6)


def bit_of(me, stride):
    return lax.rem(lax.div(me, stride), 2)


def other(me, stride):
    return me + stride * (1 - 2 * bit_of(me, stride))


ROWS, COLS, TOKENS, TILE = 1024, 2560, 2048, 512
TILES = COLS // TILE
HALF, WIDTH = ROWS // 2, COLS // 4


def gradients_kernel(which, n, *refs):
    k = len(which)
    units = [(i, c) for i in range(k) for c in range(2)]
    count = max(which) + 1
    lhs, rhs, outs, sq_out = refs[:count], refs[count : count + k], refs[count + k : count + 2 * k], refs[count + 2 * k]
    refs = refs[count + 2 * k + 1 :]
    own, landed, refs = refs[:k], [refs[k + 5 * i : k + 5 * i + 5] for i in range(k)], refs[6 * k :]
    final, (sq, raw, turned, right, away) = refs[:k], refs[k : k + 5]
    raw_sem, right_sem, core_send, core_recv, send_sem, recv_sem, ag_local, ag_send, ag_recv, sq_send, sq_recv = refs[k + 5 :]
    me = lax.axis_index("dp")
    core = bit_of(me, CORE)

    def remote(src, dst, send, recv, stride):
        return pltpu.make_async_remote_copy(src, dst, send, recv, device_id={"dp": other(me, stride)}, device_id_type=MESH)

    def columns(unit, half):
        return pl.ds(unit[1] * 2 * WIDTH + half * WIDTH, WIDTH)

    def starts(half):
        size, at = HALF, 0
        found = [at]
        for stride in ORDERS[half]:
            size //= 2
            at = at + bit_of(me, stride) * size
            found.append(at)
        return found

    def raw_copy(index):
        return pltpu.make_async_copy(lhs[index], raw, raw_sem)

    def right_copy(i, j):
        slot = lax.rem(i * TILES + j, 2)
        cols = pl.ds(pl.multiple_of(j * TILE, TILE), TILE)
        return pltpu.make_async_copy(rhs[i].at[:, cols], right.at[slot], right_sem.at[slot])

    def core_copy(i, j):
        cols = pl.ds(pl.multiple_of(j * TILE, TILE), TILE)
        return remote(away.at[lax.rem(j, 2)], landed[i][0].at[:, cols], core_send.at[i, j], core_recv.at[i, j], CORE)

    def rs_copy(unit, half, stage):
        stride = ORDERS[half][stage - 1]
        size = ROWS >> (stage + 1)
        at = starts(half)[stage - 1] + (1 - bit_of(me, stride)) * size
        cols = columns(unit, half)
        return remote(
            own[unit[0]].at[pl.ds(pl.multiple_of(at, 16), size), cols],
            landed[unit[0]][stage].at[:, cols],
            send_sem.at[units.index(unit), half, stage],
            recv_sem.at[units.index(unit), half, stage],
            stride,
        )

    def summed(unit, half, stage, at, row):
        cols, found = columns(unit, half), starts(half)
        place = lambda start: pl.ds(pl.multiple_of(at - start + row, 16), 16)
        total = own[unit[0]][place(0), cols].astype(jnp.float32)
        for s in range(stage + 1):
            total += landed[unit[0]][s][place(found[s]), cols].astype(jnp.float32)
        return total

    def rs_step(unit, half, stage):
        stride = ORDERS[half][stage - 1]
        size = ROWS >> (stage + 1)
        at = starts(half)[stage - 1] + (1 - bit_of(me, stride)) * size

        @pl.loop(0, size // 16)
        def _(block):
            row = block * 16
            total = summed(unit, half, stage - 1, at, row)
            own[unit[0]][pl.ds(pl.multiple_of(at + row, 16), 16), columns(unit, half)] = total.astype(jnp.bfloat16)

        rs_copy(unit, half, stage).start()

    def finish(unit, half):
        at = starts(half)[4]

        @pl.loop(0, ROWS // 32 // 16)
        def _(block):
            row = block * 16
            total = summed(unit, half, 4, at, row).astype(jnp.bfloat16)
            final[unit[0]][pl.ds(pl.multiple_of(row, 16), 16), columns(unit, half)] = total
            wide = total.astype(jnp.float32)
            wide = wide * wide
            part = wide[:, :128]
            for j in range(1, WIDTH // 128):
                part += wide[:, j * 128 : (j + 1) * 128]
            sq[...] += part

    def region(unit, half, stage):
        at = core * HALF + starts(half)[stage]
        return pl.ds(pl.multiple_of(at, 16), ROWS >> (stage + 1)), columns(unit, half)

    def ag_copy(unit, half, stage):
        rows, cols = region(unit, half, stage)
        src = final[unit[0]].at[:, cols] if stage == 4 else outs[unit[0]].at[rows, cols]
        return remote(
            src, outs[unit[0]].at[rows, cols], ag_send.at[units.index(unit), half, stage], ag_recv.at[units.index(unit), half, stage], ORDERS[half][stage - 1]
        )

    def ag_own(unit, half):
        rows, cols = region(unit, half, 4)
        return pltpu.make_async_copy(final[unit[0]].at[:, cols], outs[unit[0]].at[rows, cols], ag_local.at[units.index(unit), half])

    def ag_core(unit):
        mine, cols = pl.ds(pl.multiple_of(core * HALF, 16), HALF), pl.ds(unit[1] * 2 * WIDTH, 2 * WIDTH)
        place, number = outs[unit[0]].at[mine, cols], units.index(unit)
        return remote(place, place, ag_send.at[number, 0, 0], ag_recv.at[number, 0, 0], CORE)

    def advance(unit, step):
        if step == 0:
            for j in range(3) if unit[1] == 0 else range(3, TILES):
                core_copy(unit[0], j).wait_recv()
        if step < 4:
            for half in range(2):
                if step:
                    rs_copy(unit, half, step).wait_recv()
                rs_step(unit, half, step + 1)
        elif step == 4:
            for half in range(2):
                rs_copy(unit, half, 4).wait_recv()
                finish(unit, half)
                ag_copy(unit, half, 4).start()
                ag_own(unit, half).start()
        elif step < 8:
            for half in range(2):
                if step == 5:
                    ag_own(unit, half).wait()
                ag_copy(unit, half, 9 - step).wait_recv()
                ag_copy(unit, half, 8 - step).start()
        elif step == 8:
            for half in range(2):
                ag_copy(unit, half, 1).wait_recv()
            ag_core(unit).start()
        else:
            ag_core(unit).wait_recv()

    def sq_copy(hops):
        to = lax.rem(me + hops, n)
        return pltpu.make_async_remote_copy(
            sq, sq_out.at[me], sq_send.at[hops], sq_recv.at[hops], device_id={"dp": to}, device_id_type=MESH
        )

    def turn_lhs():
        @pl.loop(0, TOKENS // 128)
        def _(block):
            at = pl.ds(pl.multiple_of(block * 128, 128), 128)
            turned[:, at] = raw[at, :].T

    def product(i, j):
        slot = lax.rem(i * TILES + j, 2)
        right_copy(i, j).wait()

        @pl.when(j + 1 < TILES)
        def _():
            right_copy(i, j + 1).start()

        if i + 1 < k:

            @pl.when(j + 1 == TILES)
            def _():
                right_copy(i + 1, 0).start()

        half = lambda which: turned[pl.ds(pl.multiple_of(which * HALF, HALF), HALF), :]
        dot = lambda a: jnp.dot(a, right[slot], preferred_element_type=jnp.float32).astype(jnp.bfloat16)
        away[lax.rem(j, 2)] = dot(half(1 - core))
        core_copy(i, j).start()
        own[i][:, pl.ds(pl.multiple_of(j * TILE, TILE), TILE)] = dot(half(core))

        @pl.when(j >= 1)
        def _():
            core_copy(i, j - 1).wait_send()

    def due(turn):
        return [(units[turn - 1 - step], step) for step in range(10) if 0 <= turn - 1 - step < len(units)]

    def share(some, part, parts):
        size = -(-len(some) // parts)
        return some[part * size : (part + 1) * size]

    raw_copy(which[0]).start()
    right_copy(0, 0).start()
    sq[...] = jnp.zeros_like(sq)
    for t in range(k):
        if t == 0 or which[t] != which[t - 1]:
            raw_copy(which[t]).wait()
            turn_lhs()
            if which[t] + 1 < count:
                raw_copy(which[t] + 1).start()

        @pl.loop(0, TILES)
        def _(j):
            product(t, j)
            for place in range(TILES):
                some = share(due(2 * t), place, 3) if place < 3 else share(due(2 * t + 1), place - 3, 2)
                if some:

                    @pl.when(j == place)
                    def _():
                        for unit, step in some:
                            advance(unit, step)

        core_copy(t, TILES - 1).wait_send()

    for turn in range(2 * k, 2 * k + 10):
        for unit, step in due(turn):
            advance(unit, step)
            if step == 4 and unit == units[-1]:
                sq_out[me] = sq[...]

                @pl.loop(1, n)
                def _(hops):
                    sq_copy(hops).start()

    @pl.loop(1, n)
    def _(hops):
        sq_copy(hops).wait()

    for unit in units:
        ag_core(unit).wait_send()
        for half in range(2):
            for stage in range(1, 5):
                rs_copy(unit, half, stage).wait_send()
                ag_copy(unit, half, stage).wait_send()


def gradients(lhs, rhs, which, n):
    k = len(which)
    vmem = lambda *shape: pltpu.VMEM(shape, jnp.bfloat16)
    scratch = [vmem(HALF, COLS)] * k + [vmem(ROWS >> (stage + 1), COLS) for stage in range(5)] * k + [vmem(ROWS // 32, COLS)] * k
    scratch += [pltpu.VMEM((16, 128), jnp.float32), vmem(TOKENS, ROWS), vmem(ROWS, TOKENS), vmem(2, TOKENS, TILE), vmem(2, HALF, TILE)]
    dma = pltpu.SemaphoreType.DMA
    scratch += [dma, dma((2,)), dma((k, TILES)), dma((k, TILES)), dma((2 * k, 2, 5)), dma((2 * k, 2, 5))]
    scratch += [dma((2 * k, 2)), dma((2 * k, 2, 5)), dma((2 * k, 2, 5)), dma((n,)), dma((n,))]
    return pl.pallas_call(
        functools.partial(gradients_kernel, which, n),
        out_shape=[jax.ShapeDtypeStruct((ROWS, COLS), jnp.bfloat16)] * k + [jax.ShapeDtypeStruct((n, 16, 128), jnp.float32)],
        in_specs=[pl.BlockSpec(memory_space=pl.ANY)] * (len(lhs) + k),
        out_specs=[pl.BlockSpec(memory_space=pl.ANY)] * k + [pl.BlockSpec(memory_space=pltpu.VMEM)],
        scratch_shapes=scratch,
        compiler_params=pltpu.CompilerParams(has_side_effects=True, vmem_limit_bytes=LIMIT),
        cost_estimate=pl.CostEstimate(flops=2 * k * TOKENS * ROWS * COLS, bytes_accessed=10**8, transcendentals=0),
        name="gradients",
    )(*lhs, *rhs)


PART, CHUNK, STRIP = 512, 512, 256
PARTS = COLS // PART
CHUNKS = [pl.ds(r * CHUNK, CHUNK) for r in range(TOKENS // CHUNK)]


def forward_kernel(x_hbm, w_gate, w_up, w_down, gate_out, up_out, act_out, a_hbm, h_hbm, next_hbm, h, a, total, sem):
    j = pl.program_id(0)
    keep_a = pltpu.make_async_copy(a, a_hbm, sem.at[1])

    @pl.when(j == 0)
    def _():
        load = pltpu.make_async_copy(x_hbm, h, sem.at[0])
        load.start()
        load.wait()
        total[...] = jnp.zeros_like(total)

        @pl.loop(0, TOKENS // STRIP)
        def _(block):
            rows = pl.ds(pl.multiple_of(block * STRIP, STRIP), STRIP)
            wide = h[rows, :].astype(jnp.float32)
            a[rows, :] = (wide * scale_of(wide)).astype(jnp.bfloat16)

        keep_a.start()

    for rows in CHUNKS:
        gate, up = f32dot(a[rows, :], w_gate[...]), f32dot(a[rows, :], w_up[...])
        act = (gate * jax.nn.sigmoid(gate) * up).astype(jnp.bfloat16)
        gate_out[rows, :] = gate
        up_out[rows, :] = up
        act_out[rows, :] = act
        total[rows, :] += f32dot(act, w_down[...])

    @pl.when(j == PARTS - 1)
    def _():
        keep_a.wait()

        @pl.loop(0, TOKENS // STRIP)
        def _(block):
            rows = pl.ds(pl.multiple_of(block * STRIP, STRIP), STRIP)
            new = h[rows, :] + total[rows, :].astype(jnp.bfloat16)
            h[rows, :] = new
            wide = new.astype(jnp.float32)
            a[rows, :] = (wide * scale_of(wide)).astype(jnp.bfloat16)

        copies = [pltpu.make_async_copy(h, h_hbm, sem.at[0]), pltpu.make_async_copy(a, next_hbm, sem.at[1])]
        for copy in copies:
            copy.start()
        for copy in copies:
            copy.wait()


def hidden_gradients(gate, up, by_act):
    by_act = by_act.astype(jnp.bfloat16).astype(jnp.float32)
    sig = jax.nn.sigmoid(gate)
    silu = gate * sig
    by_gate = by_act * up * (sig + silu * (1 - sig))
    return (silu * up).astype(jnp.bfloat16), by_gate.astype(jnp.bfloat16), (by_act * silu).astype(jnp.bfloat16)


def top_kernel(
    a_hbm, by_hbm, h_hbm, w_gate, w_up, w_down, act_out, by_gate_out, by_up_out, by_h_hbm, a, by, h, total, sem
):
    j = pl.program_id(0)
    load_h = pltpu.make_async_copy(h_hbm, h, sem.at[2])

    @pl.when(j == 0)
    def _():
        loads = [pltpu.make_async_copy(a_hbm, a, sem.at[0]), pltpu.make_async_copy(by_hbm, by, sem.at[1])]
        for load in loads:
            load.start()
        load_h.start()
        total[...] = jnp.zeros_like(total)
        for load in loads:
            load.wait()

    for rows in CHUNKS:
        gate, up = f32dot(a[rows, :], w_gate[...]), f32dot(a[rows, :], w_up[...])
        act, by_gate, by_up = hidden_gradients(gate, up, f32dot(by[rows, :], w_down[...], 1))
        act_out[rows, :] = act
        by_gate_out[rows, :] = by_gate
        by_up_out[rows, :] = by_up
        total[rows, :] += f32dot(by_gate, w_gate[...], 1) + f32dot(by_up, w_up[...], 1)

    @pl.when(j == PARTS - 1)
    def _():
        load_h.wait()

        @pl.loop(0, TOKENS // STRIP)
        def _(block):
            rows = pl.ds(pl.multiple_of(block * STRIP, STRIP), STRIP)
            by_a = total[rows, :].astype(jnp.bfloat16).astype(jnp.float32)
            wide = h[rows, :].astype(jnp.float32)
            scale = scale_of(wide)
            by_scale = jnp.sum(by_a * wide, -1, keepdims=True)
            by_wide = by_a * scale - wide * (scale * scale * scale * by_scale * (1 / ROWS))
            by[rows, :] = by[rows, :] + by_wide.astype(jnp.bfloat16)

        store = pltpu.make_async_copy(by, by_h_hbm, sem.at[0])
        store.start()
        store.wait()


def bottom_kernel(by, w_down, gate, up, by_gate_out, by_up_out):
    for rows in CHUNKS:
        _, by_gate, by_up = hidden_gradients(gate[rows, :], up[rows, :], f32dot(by[rows, :], w_down[...], 1))
        by_gate_out[rows, :] = by_gate
        by_up_out[rows, :] = by_up


def wide_part(number):
    return pl.BlockSpec((None, ROWS, PART), lambda j: (number, 0, j))


def tall_part(number):
    return pl.BlockSpec((None, PART, ROWS), lambda j: (number, j, 0))


ANY = pl.BlockSpec(memory_space=pl.ANY)
HIDDEN = pl.BlockSpec((TOKENS, PART), lambda j: (0, j))


def layer_call(kernel, matmuls, in_specs, out_specs, outs, scratch, name):
    return pl.pallas_call(
        kernel,
        grid=(PARTS,),
        out_shape=[jax.ShapeDtypeStruct(shape, dtype) for shape, dtype in outs],
        in_specs=in_specs,
        out_specs=out_specs,
        scratch_shapes=scratch,
        compiler_params=pltpu.CompilerParams(vmem_limit_bytes=LIMIT, dimension_semantics=("arbitrary",)),
        cost_estimate=pl.CostEstimate(flops=2 * matmuls * TOKENS * ROWS * COLS, bytes_accessed=10**8, transcendentals=TOKENS * COLS),
        name=name,
    )


def forward(x, w_gate, w_up, w_down):
    tokens, hidden = (TOKENS, ROWS), (TOKENS, COLS)
    outs = [(hidden, jnp.float32)] * 2 + [(hidden, jnp.bfloat16)] + [(tokens, jnp.bfloat16)] * 3
    scratch = [pltpu.VMEM(tokens, jnp.bfloat16)] * 2 + [pltpu.VMEM(tokens, jnp.float32), pltpu.SemaphoreType.DMA((2,))]
    specs = [ANY, wide_part(0), wide_part(0), tall_part(0)], [HIDDEN] * 3 + [ANY] * 3
    return layer_call(forward_kernel, 3, *specs, outs, scratch, "forward")(x, w_gate, w_up, w_down)


def top(a, by, h, w_gate, w_up, w_down):
    tokens, hidden = (TOKENS, ROWS), (TOKENS, COLS)
    outs = [(hidden, jnp.bfloat16)] * 3 + [(tokens, jnp.bfloat16)]
    scratch = [pltpu.VMEM(tokens, jnp.bfloat16)] * 3 + [pltpu.VMEM(tokens, jnp.float32), pltpu.SemaphoreType.DMA((3,))]
    specs = [ANY] * 3 + [wide_part(1), wide_part(1), tall_part(1)], [HIDDEN] * 3 + [ANY]
    return layer_call(top_kernel, 5, *specs, outs, scratch, "top")(a, by, h, w_gate, w_up, w_down)


def bottom(by, w_down, gate, up):
    outs = [((TOKENS, COLS), jnp.bfloat16)] * 2
    whole = pl.BlockSpec((TOKENS, ROWS), lambda j: (0, 0))
    return layer_call(bottom_kernel, 1, [whole, tall_part(0), HIDDEN, HIDDEN], [HIDDEN] * 2, outs, [], "bottom")(by, w_down, gate, up)


def adamw_kernel(turned, factor_ref, g0_ref, g1_ref, w_ref, m_ref, v_ref, w_out, m_out, v_out):
    factor = factor_ref[0, 0]

    rows = w_ref.shape[1]
    strip = 128 if turned else 16

    def update(g_ref):
        @pl.loop(0, rows // strip)
        def _(block):
            at = pl.ds(pl.multiple_of(block * strip, strip), strip)
            g = (g_ref[:, at].astype(jnp.float32).T if turned else g_ref[at, :].astype(jnp.float32)) * factor
            m = 0.9 * m_ref[0, at] + 0.1 * g
            v = 0.95 * v_ref[0, at] + 0.05 * g * g
            w = w_ref[0, at].astype(jnp.float32)
            step = m * lax.rsqrt(v + 1e-8) + 0.1 * w
            w_out[0, at] = (w - 0.02 * step).astype(jnp.bfloat16)
            m_out[0, at] = m
            v_out[0, at] = v

    number = pl.program_id(0)

    @pl.when(number == 0)
    def _():
        update(g0_ref)

    @pl.when(number == 1)
    def _():
        update(g1_ref)


def adamw(factor, g0, g1, w, m, v, rows, turned):
    layers, r, c = w.shape
    blocks = r // rows
    whole = pl.BlockSpec((1, rows, c), lambda number, i: (number, i, 0))
    shape = (c, rows) if turned else (rows, c)
    at = lambda i: (0, i) if turned else (i, 0)
    in0 = pl.BlockSpec(shape, lambda number, i: at(jnp.where(number == 0, i, blocks - 1)))
    in1 = pl.BlockSpec(shape, lambda number, i: at(jnp.where(number == 1, i, 0)))
    return pl.pallas_call(
        functools.partial(adamw_kernel, turned),
        grid=(layers, blocks),
        out_shape=[jax.ShapeDtypeStruct(a.shape, a.dtype) for a in (w, m, v)],
        in_specs=[pl.BlockSpec((1, 1), lambda number, i: (0, 0), memory_space=pltpu.SMEM), in0, in1, whole, whole, whole],
        out_specs=[whole] * 3,
        compiler_params=pltpu.CompilerParams(vmem_limit_bytes=LIMIT, dimension_semantics=("arbitrary", "arbitrary")),
        cost_estimate=pl.CostEstimate(flops=20 * w.size, bytes_accessed=22 * w.size, transcendentals=w.size),
        name="adamw",
    )(factor, g0, g1, w, m, v)


def solution(mesh):
    n = mesh.shape["dp"]

    def step(x, dy, *arrays):
        weights, m, v = (arrays[i : i + 3] for i in (0, 3, 6))
        gate, up, act0, a0, h1, a1 = forward(x[0], *weights)
        act1, by_gate1, by_up1, by_h1 = top(a1, dy[0], h1, *weights)
        by_gate0, by_up0 = bottom(by_h1, weights[2], gate, up)
        lhs, rhs = (dy[0], a1, by_h1, a0), (act1, by_gate1, by_up1, act0, by_gate0, by_up0)
        down1, gate1, up1, down0, gate0, up0, squares = gradients(lhs, rhs, (0, 1, 1, 2, 3, 3), n)
        total = jnp.sum(squares)
        factor = jnp.minimum(1.0, 0.5 * lax.rsqrt(total / sum(w.size for w in weights) + 1e-30)).reshape(1, 1)
        pairs = ((gate0, gate1), (up0, up1), (down0, down1))
        new = [
            adamw(factor, *pair, w, m, v, rows, turned)
            for pair, w, m, v, rows, turned in zip(pairs, weights, m, v, (256, 256, 640), (False, False, True), strict=True)
        ]
        return tuple(one[which] for which in range(3) for one in new)

    return jax.shard_map(
        step,
        mesh=mesh,
        in_specs=(P(("rep", "dp"), None, None),) * 2 + (P(None, None, None),) * 9,
        out_specs=(P("rep", None, None),) * 9,
        check_vma=False,
    )
```

time: 638 us -> 547 us (0.86)
  matrix products: 199 us -> 0 us
  Pallas kernels: 413 us -> 541 us
  other arithmetic: 13.6 us -> 1.62 us
    dot_general x9 -> x0, matrix products: 199 us -> none  [f32dot(): lax.dot_general(a, w, (((1,), (over,)), ((), ())), preferred_element_type...]
    pallas_call x0 -> x3, Pallas kernels: none -> 156 us  [the longest x1 73.7 us: top(): layer_call(top_kernel, 5, *specs, outs, scratch, 'top')]
    pallas_call x1, Pallas kernels: 297 us -> 269 us  [gradients(): pl.pallas_call(functools.partial(gradients_kernel, which, n), out_shape=[...]
where the time goes in v3:
time: 547 us; the launch traced here: 544 us
  Pallas kernels  541 us (99%)
    pallas_call x1, Pallas kernels, gradients(): pl.pallas_call(functools.partial(gradients_kernel, which, n), out_shape=[...  269 us
    pallas_call x3, Pallas kernels, adamw(): pl.pallas_call(functools.partial(adamw_kernel, turned), grid=(layers, blo...  116 us
    pallas_call x1, Pallas kernels, top(): layer_call(top_kernel, 5, *specs, outs, scratch, 'top')  73.7 us
    pallas_call x1, Pallas kernels, forward(): layer_call(forward_kernel, 3, *specs, outs, scratch, 'forward')  49.7 us
    pallas_call x1, Pallas kernels, bottom(): layer_call(bottom_kernel, 1, [whole, tall_part(0), HIDDEN, HIDDEN], [HIDD...  32.2 us

profile of v3, /device:TPU:25, one launch (start us, length us, event | category | flops | bytes accessed | tf_op | source)
XLA Modules:
  0.0 543.8 jit_solution(53848416003772144)
XLA Ops:
  0.6 49.7 %forward.1 = (f32[2048,2560]{1,0:T(8,128)}, f32[2048,2560]{1,0:T(8,128)}, bf16[2048,2560]{1,0:T(8,128)(2,1)}, bf16[2048,1024]{1,0:T(8,128)(2,1)}, bf16[2048,1024...) custom-call(bf16[2048,1024]{1,0:T(8,128)(2,1)} %bitcast.3, bf16[2,1024,2560]{2,1,0:T(8,128)(2,1)} %w_ref.3, ...), custom_call_target="tpu_custom_call" | custom-call | flops 32212254720 | bytes 100000000 | tf_op jit(solution)/shard_map/forward/pallas_call | solution.py:422
  50.3 73.7 %top.1 = (bf16[2048,2560]{1,0:T(8,128)(2,1)}, bf16[2048,2560]{1,0:T(8,128)(2,1)}, bf16[2048,2560]{1,0:T(8,128)(2,1)}, bf16[2048,1024]{1,0:T(8,128)(2,1)}) custom-call(bf16[2048,1024]{1,0:T(8,128)(2,1)} %get-tuple-element.37.a_hbm.refs_1_, bf16[2048,1024]{1,0:T(8,128)(2,1)} %bitcast.4, bf16[2048,1024]{1,0:T(8,128)(2,1)} %get-tuple-element.38.h_hbm, ...), custom_call_target="tpu_custom_call" | custom-call | flops 53687091200 | bytes 100000000 | tf_op jit(solution)/shard_map/top/pallas_call | solution.py:430
  124.0 32.2 %bottom.1 = (bf16[2048,2560]{1,0:T(8,128)(2,1)}, bf16[2048,2560]{1,0:T(8,128)(2,1)}) custom-call(bf16[2048,1024]{1,0:T(8,128)(2,1)} %get-tuple-element.39.by.refs_2_, bf16[2,2560,1024]{2,1,0:T(8,128)(2,1)} %w_ref.5, f32[2048,2560]{1,0:T(8,128)} %get-tuple-element.45.gate, f32[2048,2560]{1,0:T(8,128)} %get-tuple-element.46.up), custom_call_target="tpu_custom_call" | custom-call | flops 10737418240 | bytes 100000000 | tf_op jit(solution)/shard_map/bottom/pallas_call | solution.py:436
  156.2 268.8 %gradients.1 = (bf16[1024,2560]{1,0:T(8,128)(2,1)}, bf16[1024,2560]{1,0:T(8,128)(2,1)}, bf16[1024,2560]{1,0:T(8,128)(2,1)}, bf16[1024,2560]{1,0:T(8,128)(2,1)}, ...) custom-call(bf16[2048,1024]{1,0:T(8,128)(2,1)} %bitcast.5, ...), custom_call_target="tpu_custom_call" | custom-call | flops 64424509440 | bytes 100000000 | tf_op jit(solution)/shard_map/gradients/pallas_call | solution.py:270
  425.0 1.6 reduce_sum.9
  427.3 39.5 %adamw.5 = (bf16[2,2560,1024]{2,1,0:T(8,128)(2,1)}, f32[2,2560,1024]{2,1,0:T(8,128)}, f32[2,2560,1024]{2,1,0:T(8,128)}) custom-call(f32[1,1]{1,0:T(1,128)} %bitcast.2.factor_ref, bf16[1024,2560]{1,0:T(8,128)(2,1)} %get-tuple-element.56.g0_ref, bf16[1024,2560]{1,0:T(8,128)(2,1)} %get-tuple-element.57.g1_ref, bf16[2,2560,1024]{2,1,0:T(8,128)(2,1)} %w_ref.5, ...), custom_call_target="tpu_custom_call" | custom-call | flops 104857600 | bytes 115343360 | tf_op jit(solution)/shard_map/adamw/pallas_call | solution.py:477
  466.8 38.5 %adamw.4 = (bf16[2,1024,2560]{2,1,0:T(8,128)(2,1)}, f32[2,1024,2560]{2,1,0:T(8,128)}, f32[2,1024,2560]{2,1,0:T(8,128)}) custom-call(f32[1,1]{1,0:T(1,128)} %bitcast.2.factor_ref, bf16[1024,2560]{1,0:T(8,128)(2,1)} %get-tuple-element.53.g0_ref, bf16[1024,2560]{1,0:T(8,128)(2,1)} %get-tuple-element.54.g1_ref, bf16[2,1024,2560]{2,1,0:T(8,128)(2,1)} %w_ref.4, ...), custom_call_target="tpu_custom_call" | custom-call | flops 104857600 | bytes 115343360 | tf_op jit(solution)/shard_map/adamw/pallas_call | solution.py:477
  505.3 38.5 %adamw.3 = (bf16[2,1024,2560]{2,1,0:T(8,128)(2,1)}, f32[2,1024,2560]{2,1,0:T(8,128)}, f32[2,1024,2560]{2,1,0:T(8,128)}) custom-call(f32[1,1]{1,0:T(1,128)} %bitcast.2.factor_ref, bf16[1024,2560]{1,0:T(8,128)(2,1)} %get-tuple-element.50.g0_ref, bf16[1024,2560]{1,0:T(8,128)(2,1)} %get-tuple-element.51.g1_ref, bf16[2,1024,2560]{2,1,0:T(8,128)(2,1)} %w_ref.3, ...), custom_call_target="tpu_custom_call" | custom-call | flops 104857600 | bytes 115343360 | tf_op jit(solution)/shard_map/adamw/pallas_call | solution.py:477

commit v4 on v3

--- a/solution.py
+++ b/solution.py
@@ -8,7 +8,7 @@
 from jax.sharding import PartitionSpec as P
 
 MESH = pl.DeviceIdType.MESH
-LIMIT = 66_000_000
+LIMIT = 67_000_000
 CORE, Z1, Z2, Y, X = 1, 2, 4, 8, 16
 ORDERS = ((X, Z1, Y, Z2), (Y, Z1, X, Z2))
 
@@ -32,17 +32,21 @@
 ROWS, COLS, TOKENS, TILE = 1024, 2560, 2048, 512
 TILES = COLS // TILE
 HALF, WIDTH = ROWS // 2, COLS // 4
+LATE, LATE_ROWS = 4, 256
+CHUNKS_LATE = TOKENS // LATE_ROWS
 
 
 def gradients_kernel(which, n, *refs):
     k = len(which)
     units = [(i, c) for i in range(k) for c in range(2)]
     count = max(which) + 1
-    lhs, rhs, outs, sq_out = refs[:count], refs[count : count + k], refs[count + k : count + 2 * k], refs[count + 2 * k]
-    refs = refs[count + 2 * k + 1 :]
+    lhs, rhs, (gates, ups, w_down), refs = refs[:count], refs[count : count + k - 2], refs[count + k - 2 : count + k + 1], refs[count + k + 1 :]
+    outs, sq_out, by_hidden, refs = refs[:k], refs[k], refs[k + 1 : k + 3], refs[k + 3 :]
+    rhs += by_hidden
     own, landed, refs = refs[:k], [refs[k + 5 * i : k + 5 * i + 5] for i in range(k)], refs[6 * k :]
-    final, (sq, raw, turned, right, away) = refs[:k], refs[k : k + 5]
-    raw_sem, right_sem, core_send, core_recv, send_sem, recv_sem, ag_local, ag_send, ag_recv, sq_send, sq_recv = refs[k + 5 :]
+    final, (sq, raw, turned, right, away, projected) = refs[:k], refs[k : k + 6]
+    raw_sem, right_sem, core_send, core_recv, send_sem, recv_sem, ag_local, ag_send, ag_recv, sq_send, sq_recv = refs[k + 6 : k + 17]
+    w_sem, in_sem, out_sem = refs[k + 17 :]
     me = lax.axis_index("dp")
     core = bit_of(me, CORE)
 
@@ -190,7 +194,7 @@
         def _():
             right_copy(i, j + 1).start()
 
-        if i + 1 < k:
+        if i + 1 < k and i + 1 != LATE:
 
             @pl.when(j + 1 == TILES)
             def _():
@@ -206,8 +210,95 @@
         def _():
             core_copy(i, j - 1).wait_send()
 
+    def w_copies(part):
+        slot, rows = lax.rem(part, 2), pl.ds(pl.multiple_of(part * TILE, TILE), TILE)
+        return [
+            pltpu.make_async_copy(
+                w_down.at[0, rows, pl.ds(d * TILE, TILE)], right.at[slot, pl.ds(d * TILE, TILE), :], w_sem.at[slot, d]
+            )
+            for d in range(ROWS // TILE)
+        ]
+
+    def place_of(q):
+        part, chunk = lax.div(q, CHUNKS_LATE), lax.rem(q, CHUNKS_LATE)
+        return pl.ds(pl.multiple_of(chunk * LATE_ROWS, LATE_ROWS), LATE_ROWS), pl.ds(pl.multiple_of(part * TILE, TILE), TILE)
+
+    def in_copies(q):
+        slot, place = lax.rem(q, 2), place_of(q)
+        return [pltpu.make_async_copy(ref.at[place], projected.at[slot, d], in_sem.at[slot, d]) for d, ref in enumerate((gates, ups))]
+
+    def out_copies(q):
+        slot, place = lax.rem(q, 2), place_of(q)
+        return [
+            pltpu.make_async_copy(away.at[slot, pl.ds(d * LATE_ROWS, LATE_ROWS), :], ref.at[place], out_sem.at[slot, d])
+            for d, ref in enumerate(by_hidden)
+        ]
+
+    def start(copies):
+        for copy in copies:
+            copy.start()
+
+    def wait(copies):
+        for copy in copies:
+            copy.wait()
+
+    def late(q, number):
+        part, chunk, slot = lax.div(q, CHUNKS_LATE), lax.rem(q, CHUNKS_LATE), lax.rem(q, 2)
+        wait(in_copies(q))
+
+        @pl.when(q + 1 < number)
+        def _():
+            start(in_copies(q + 1))
+
+        @pl.when(chunk == 0)
+        def _():
+            wait(w_copies(part))
+
+            @pl.when(part + 1 < TILES)
+            def _():
+                start(w_copies(part + 1))
+
+        @pl.when(q >= 2)
+        def _():
+            wait(out_copies(q - 2))
+
+        rows = pl.ds(pl.multiple_of(chunk * LATE_ROWS, LATE_ROWS), LATE_ROWS)
+        w = right.at[lax.rem(part, 2)]
+        for side in range(2):
+            cols = pl.ds(side * (TILE // 2), TILE // 2)
+            by_act = sum(
+                f32dot(raw[rows, pl.ds(d * TILE, TILE)], w[pl.ds(d * TILE + side * (TILE // 2), TILE // 2), :], 1)
+                for d in range(ROWS // TILE)
+            )
+            _, by_gate, by_up = hidden_gradients(projected[slot, 0, :, cols], projected[slot, 1, :, cols], by_act)
+            away[slot, pl.ds(0, LATE_ROWS), cols] = by_gate
+            away[slot, pl.ds(LATE_ROWS, LATE_ROWS), cols] = by_up
+        start(out_copies(q))
+
+    def late_phase(first, second):
+        number = TILES * CHUNKS_LATE
+        start(w_copies(0))
+        start(in_copies(0))
+
+        @pl.loop(0, number)
+        def _(q):
+            late(q, number)
+            for place, some in [(part * number // 6, share(first, part, 3)) for part in range(3)] + [
+                ((part + 3) * number // 6, share(second, part, 3)) for part in range(3)
+            ]:
+                if some:
+
+                    @pl.when(q == place)
+                    def _():
+                        for unit, step in some:
+                            advance(unit, step)
+
+        wait(out_copies(number - 2))
+        wait(out_copies(number - 1))
+
     def due(turn):
-        return [(units[turn - 1 - step], step) for step in range(10) if 0 <= turn - 1 - step < len(units)]
+        ready = [u + 1 + 2 * (u >= 2 * LATE) for u in range(len(units))]
+        return [(units[u], turn - ready[u]) for u in reversed(range(len(units))) if 0 <= turn - ready[u] < 10]
 
     def share(some, part, parts):
         size = -(-len(some) // parts)
@@ -217,17 +308,22 @@
     right_copy(0, 0).start()
     sq[...] = jnp.zeros_like(sq)
     for t in range(k):
+        turn = 2 * t + 2 * (t >= LATE)
+        if t == LATE:
+            late_phase(due(turn - 2), due(turn - 1))
+            raw_copy(which[t]).start()
+            right_copy(t, 0).start()
         if t == 0 or which[t] != which[t - 1]:
             raw_copy(which[t]).wait()
             turn_lhs()
-            if which[t] + 1 < count:
+            if which[t] + 1 < count and t + 1 != LATE:
                 raw_copy(which[t] + 1).start()
 
         @pl.loop(0, TILES)
         def _(j):
             product(t, j)
             for place in range(TILES):
-                some = share(due(2 * t), place, 3) if place < 3 else share(due(2 * t + 1), place - 3, 2)
+                some = share(due(turn), place, 3) if place < 3 else share(due(turn + 1), place - 3, 2)
                 if some:
 
                     @pl.when(j == place)
@@ -237,7 +333,7 @@
 
         core_copy(t, TILES - 1).wait_send()
 
-    for turn in range(2 * k, 2 * k + 10):
+    for turn in range(2 * k + 2, 2 * k + 12):
         for unit, step in due(turn):
             advance(unit, step)
             if step == 4 and unit == units[-1]:
@@ -259,24 +355,27 @@
                 ag_copy(unit, half, stage).wait_send()
 
 
-def gradients(lhs, rhs, which, n):
+def gradients(lhs, rhs, gate, up, w_down, which, n):
     k = len(which)
     vmem = lambda *shape: pltpu.VMEM(shape, jnp.bfloat16)
     scratch = [vmem(HALF, COLS)] * k + [vmem(ROWS >> (stage + 1), COLS) for stage in range(5)] * k + [vmem(ROWS // 32, COLS)] * k
     scratch += [pltpu.VMEM((16, 128), jnp.float32), vmem(TOKENS, ROWS), vmem(ROWS, TOKENS), vmem(2, TOKENS, TILE), vmem(2, HALF, TILE)]
+    scratch += [pltpu.VMEM((2, 2, LATE_ROWS, TILE), jnp.float32)]
     dma = pltpu.SemaphoreType.DMA
     scratch += [dma, dma((2,)), dma((k, TILES)), dma((k, TILES)), dma((2 * k, 2, 5)), dma((2 * k, 2, 5))]
     scratch += [dma((2 * k, 2)), dma((2 * k, 2, 5)), dma((2 * k, 2, 5)), dma((n,)), dma((n,))]
+    scratch += [dma((2, 2)), dma((2, 2)), dma((2, 2))]
     return pl.pallas_call(
         functools.partial(gradients_kernel, which, n),
-        out_shape=[jax.ShapeDtypeStruct((ROWS, COLS), jnp.bfloat16)] * k + [jax.ShapeDtypeStruct((n, 16, 128), jnp.float32)],
-        in_specs=[pl.BlockSpec(memory_space=pl.ANY)] * (len(lhs) + k),
-        out_specs=[pl.BlockSpec(memory_space=pl.ANY)] * k + [pl.BlockSpec(memory_space=pltpu.VMEM)],
+        out_shape=[jax.ShapeDtypeStruct((ROWS, COLS), jnp.bfloat16)] * k + [jax.ShapeDtypeStruct((n, 16, 128), jnp.float32)]
+        + [jax.ShapeDtypeStruct((TOKENS, COLS), jnp.bfloat16)] * 2,
+        in_specs=[pl.BlockSpec(memory_space=pl.ANY)] * (len(lhs) + k + 1),
+        out_specs=[pl.BlockSpec(memory_space=pl.ANY)] * k + [pl.BlockSpec(memory_space=pltpu.VMEM)] + [pl.BlockSpec(memory_space=pl.ANY)] * 2,
         scratch_shapes=scratch,
         compiler_params=pltpu.CompilerParams(has_side_effects=True, vmem_limit_bytes=LIMIT),
         cost_estimate=pl.CostEstimate(flops=2 * k * TOKENS * ROWS * COLS, bytes_accessed=10**8, transcendentals=0),
         name="gradients",
-    )(*lhs, *rhs)
+    )(*lhs, *rhs, gate, up, w_down)[: k + 1]
 
 
 PART, CHUNK, STRIP = 512, 512, 256
@@ -379,13 +478,6 @@
         store = pltpu.make_async_copy(by, by_h_hbm, sem.at[0])
         store.start()
         store.wait()
-
-
-def bottom_kernel(by, w_down, gate, up, by_gate_out, by_up_out):
-    for rows in CHUNKS:
-        _, by_gate, by_up = hidden_gradients(gate[rows, :], up[rows, :], f32dot(by[rows, :], w_down[...], 1))
-        by_gate_out[rows, :] = by_gate
-        by_up_out[rows, :] = by_up
 
 
 def wide_part(number):
@@ -428,12 +520,6 @@
     scratch = [pltpu.VMEM(tokens, jnp.bfloat16)] * 3 + [pltpu.VMEM(tokens, jnp.float32), pltpu.SemaphoreType.DMA((3,))]
     specs = [ANY] * 3 + [wide_part(1), wide_part(1), tall_part(1)], [HIDDEN] * 3 + [ANY]
     return layer_call(top_kernel, 5, *specs, outs, scratch, "top")(a, by, h, w_gate, w_up, w_down)
-
-
-def bottom(by, w_down, gate, up):
-    outs = [((TOKENS, COLS), jnp.bfloat16)] * 2
-    whole = pl.BlockSpec((TOKENS, ROWS), lambda j: (0, 0))
-    return layer_call(bottom_kernel, 1, [whole, tall_part(0), HIDDEN, HIDDEN], [HIDDEN] * 2, outs, [], "bottom")(by, w_down, gate, up)
 
 
 def adamw_kernel(turned, factor_ref, g0_ref, g1_ref, w_ref, m_ref, v_ref, w_out, m_out, v_out):
@@ -493,9 +579,8 @@
         weights, m, v = (arrays[i : i + 3] for i in (0, 3, 6))
         gate, up, act0, a0, h1, a1 = forward(x[0], *weights)
         act1, by_gate1, by_up1, by_h1 = top(a1, dy[0], h1, *weights)
-        by_gate0, by_up0 = bottom(by_h1, weights[2], gate, up)
-        lhs, rhs = (dy[0], a1, by_h1, a0), (act1, by_gate1, by_up1, act0, by_gate0, by_up0)
-        down1, gate1, up1, down0, gate0, up0, squares = gradients(lhs, rhs, (0, 1, 1, 2, 3, 3), n)
+        lhs, rhs = (dy[0], a1, by_h1, a0), (act1, by_gate1, by_up1, act0)
+        down1, gate1, up1, down0, gate0, up0, squares = gradients(lhs, rhs, gate, up, weights[2], (0, 1, 1, 2, 3, 3), n)
         total = jnp.sum(squares)
         factor = jnp.minimum(1.0, 0.5 * lax.rsqrt(total / sum(w.size for w in weights) + 1e-30)).reshape(1, 1)
         pairs = ((gate0, gate1), (up0, up1), (down0, down1))

time: 547 us -> 533 us (0.974)
  Pallas kernels: 541 us -> 525 us
    pallas_call x1 -> x0, Pallas kernels: 32.2 us -> none  [bottom(): layer_call(bottom_kernel, 1, [whole, tall_part(0), HIDDEN, HIDDEN], [HIDD...]
    pallas_call x1, Pallas kernels: 269 us -> 285 us  [gradients(): pl.pallas_call(functools.partial(gradients_kernel, which, n), out_shape=[...]
where the time goes in v4:
time: 533 us; the launch traced here: 527 us
  Pallas kernels  525 us (98%)
    pallas_call x1, Pallas kernels, gradients(): pl.pallas_call(functools.partial(gradients_kernel, which, n), out_shape=[...  285 us
    pallas_call x3, Pallas kernels, adamw(): pl.pallas_call(functools.partial(adamw_kernel, turned), grid=(layers, blo...  116 us
    pallas_call x1, Pallas kernels, top(): layer_call(top_kernel, 5, *specs, outs, scratch, 'top')  73.7 us
    pallas_call x1, Pallas kernels, forward(): layer_call(forward_kernel, 3, *specs, outs, scratch, 'forward')  49.7 us

profile of v4, /device:TPU:25, one launch (start us, length us, event | category | flops | bytes accessed | tf_op | source)
XLA Modules:
  0.0 527.5 jit_solution(95416836539320640)
XLA Ops:
  0.6 49.7 %forward.1 = (f32[2048,2560]{1,0:T(8,128)}, f32[2048,2560]{1,0:T(8,128)}, bf16[2048,2560]{1,0:T(8,128)(2,1)}, bf16[2048,1024]{1,0:T(8,128)(2,1)}, bf16[2048,1024...) custom-call(bf16[2048,1024]{1,0:T(8,128)(2,1)} %bitcast.3, bf16[2,1024,2560]{2,1,0:T(8,128)(2,1)} %w_ref.3, ...), custom_call_target="tpu_custom_call" | custom-call | flops 32212254720 | bytes 100000000 | tf_op jit(solution)/shard_map/forward/pallas_call | solution.py:514
  50.4 73.7 %top.1 = (bf16[2048,2560]{1,0:T(8,128)(2,1)}, bf16[2048,2560]{1,0:T(8,128)(2,1)}, bf16[2048,2560]{1,0:T(8,128)(2,1)}, bf16[2048,1024]{1,0:T(8,128)(2,1)}) custom-call(bf16[2048,1024]{1,0:T(8,128)(2,1)} %get-tuple-element.35.a_hbm.refs_1_, bf16[2048,1024]{1,0:T(8,128)(2,1)} %bitcast.4, bf16[2048,1024]{1,0:T(8,128)(2,1)} %get-tuple-element.36.h_hbm, ...), custom_call_target="tpu_custom_call" | custom-call | flops 53687091200 | bytes 100000000 | tf_op jit(solution)/shard_map/top/pallas_call | solution.py:522
  124.0 284.7 %gradients.1 = (bf16[1024,2560]{1,0:T(8,128)(2,1)}, bf16[1024,2560]{1,0:T(8,128)(2,1)}, bf16[1024,2560]{1,0:T(8,128)(2,1)}, bf16[1024,2560]{1,0:T(8,128)(2,1)}, ...) custom-call(bf16[2048,1024]{1,0:T(8,128)(2,1)} %bitcast.5, ...), custom_call_target="tpu_custom_call" | custom-call | flops 64424509440 | bytes 100000000 | tf_op jit(solution)/shard_map/gradients/pallas_call | solution.py:368
  408.7 1.6 reduce_sum.9
  411.0 39.5 %adamw.5 = (bf16[2,2560,1024]{2,1,0:T(8,128)(2,1)}, f32[2,2560,1024]{2,1,0:T(8,128)}, f32[2,2560,1024]{2,1,0:T(8,128)}) custom-call(f32[1,1]{1,0:T(1,128)} %bitcast.2.factor_ref, bf16[1024,2560]{1,0:T(8,128)(2,1)} %get-tuple-element.52.g0_ref, bf16[1024,2560]{1,0:T(8,128)(2,1)} %get-tuple-element.53.g1_ref, bf16[2,2560,1024]{2,1,0:T(8,128)(2,1)} %w_ref.5, ...), custom_call_target="tpu_custom_call" | custom-call | flops 104857600 | bytes 115343360 | tf_op jit(solution)/shard_map/adamw/pallas_call | solution.py:563
  450.5 38.5 %adamw.4 = (bf16[2,1024,2560]{2,1,0:T(8,128)(2,1)}, f32[2,1024,2560]{2,1,0:T(8,128)}, f32[2,1024,2560]{2,1,0:T(8,128)}) custom-call(f32[1,1]{1,0:T(1,128)} %bitcast.2.factor_ref, bf16[1024,2560]{1,0:T(8,128)(2,1)} %get-tuple-element.49.g0_ref, bf16[1024,2560]{1,0:T(8,128)(2,1)} %get-tuple-element.50.g1_ref, bf16[2,1024,2560]{2,1,0:T(8,128)(2,1)} %w_ref.4, ...), custom_call_target="tpu_custom_call" | custom-call | flops 104857600 | bytes 115343360 | tf_op jit(solution)/shard_map/adamw/pallas_call | solution.py:563
  489.0 38.5 %adamw.3 = (bf16[2,1024,2560]{2,1,0:T(8,128)(2,1)}, f32[2,1024,2560]{2,1,0:T(8,128)}, f32[2,1024,2560]{2,1,0:T(8,128)}) custom-call(f32[1,1]{1,0:T(1,128)} %bitcast.2.factor_ref, bf16[1024,2560]{1,0:T(8,128)(2,1)} %get-tuple-element.46.g0_ref, bf16[1024,2560]{1,0:T(8,128)(2,1)} %get-tuple-element.47.g1_ref, bf16[2,1024,2560]{2,1,0:T(8,128)(2,1)} %w_ref.3, ...), custom_call_target="tpu_custom_call" | custom-call | flops 104857600 | bytes 115343360 | tf_op jit(solution)/shard_map/adamw/pallas_call | solution.py:563
